TPU v7x, 32 devices: a whole 2x2x4 slice. The times are simulated.
32 devices in a mesh: dp: 16 (over z, x, core), mp: 2 (over y).
Axes of the slice: x: 2, y: 2, z: 4, core: 2. Of those that a mesh axis runs over, the one named last changes fastest.
Arguments:
- context: bfloat16 [5120, 2048], P('dp', 'mp'), may hold values from -6 to 6
- out_weight: bfloat16 [2048, 3584], P('mp'), may hold values from -0.125 to 0.125
- cotangent: bfloat16 [5120, 3584], P('dp'), may hold values from -0.059814453 to 0.059814453
- norm_gain: float32 [3584], replicated, may hold values from 0.5 to 1.5
- first_moment: float32 [2, 1024, 3584], P('mp', 'dp'), may hold values from -6 to 6
- second_moment: float32 [2, 1024, 3584], P('mp', 'dp'), may hold values from 0.01 to 1
Outputs:
- new_weight: bfloat16 [2, 1024, 3584], P('mp', 'dp')
- new_first: float32 [2, 1024, 3584], P('mp', 'dp')
- new_second: float32 [2, 1024, 3584], P('mp', 'dp')
- grad_gain: float32 [3584], replicated
- grad_context: bfloat16 [5120, 2048], P('dp', 'mp')
All inputs are finite; a program needn't handle non-finite values.
Results may differ from a plain program's by a relative error of at most 0.005.
Values may be sent and summed in bfloat16 or wider, within the bound.
A program may use at most 128 MiB of HBM per device.

v0:
```python
import functools

import jax
import jax.numpy as jnp
from jax import lax
from jax.experimental import pallas as pl
from jax.experimental.pallas import tpu as pltpu
from jax.sharding import PartitionSpec as P

norm_floor = 0.1
learn_rate = 0.01
beta_one = 0.9
beta_two = 0.95
adam_floor = 1e-08

MESH = pl.DeviceIdType.MESH
F32 = jnp.float32
BF16 = jnp.bfloat16
LAG = 2
AHEAD = 2


def kernel(
    cfg,
    ctx_hbm, w_hbm, cot_hbm, gain_hbm, m1_hbm, m2_hbm,
    nw, n1, n2, gfin, gc_out,
    wv, ctx, ctxt_all, ctxt, cot, gain_flat, gain, psend, precv, own, stat_s, stat_r, g,
    sends, recvs, keeps, m1, m2, master, gc_acc,
    gp, gpr,
    in_sem, w_sem, cot_sem, m_sem,
    ps_s, ps_r, st_s, st_r, cx_s, cx_r, gy_s, gy_r, gm_s, gm_r,
    rs_s, rs_r, gg_s, gg_r,
):
    n, bits, half, chunks, cw, rows, tok, heads, width = cfg
    dp, mp = lax.axis_index("dp"), lax.axis_index("mp")
    peer = 1 - mp

    def flip(index, bit):
        return index + (1 << bit) * (1 - 2 * ((index // (1 << bit)) % 2))

    def peer_id():
        return (dp, peer)

    def bit_id(bit):
        return (flip(dp, bit), mp)

    def column(r):
        first = jnp.where(r < half, mp * half + r, peer * half + r - half)
        return pl.multiple_of(first * cw, cw)

    def ctx_copy():
        return pltpu.make_async_copy(ctx_hbm, ctx.at[pl.ds(0, tok)], in_sem.at[0])

    def gain_copy():
        return pltpu.make_async_copy(gain_hbm, gain_flat, in_sem.at[1])

    def w_copy(r):
        return pltpu.make_async_copy(w_hbm.at[:, pl.ds(column(r), cw)], wv.at[r], w_sem.at[r])

    def cot_copy(r):
        return pltpu.make_async_copy(cot_hbm.at[:, pl.ds(column(r), cw)], cot.at[r], cot_sem.at[r])

    def m_copies(r):
        cols = pl.ds(column(r), cw)
        return (
            pltpu.make_async_copy(m1_hbm.at[0, :, cols], m1.at[r], m_sem.at[0, r]),
            pltpu.make_async_copy(m2_hbm.at[0, :, cols], m2.at[r], m_sem.at[1, r]),
            pltpu.make_async_copy(
                w_hbm.at[pl.ds(pl.multiple_of(dp * rows, rows), rows), cols], master.at[r], m_sem.at[2, r]
            ),
        )

    def remote(src, dst, send_sem, recv_sem, device):
        return pltpu.make_async_remote_copy(
            src_ref=src, dst_ref=dst, send_sem=send_sem, recv_sem=recv_sem,
            device_id=device, device_id_type=MESH,
        )

    def partial_send(c):
        return remote(psend.at[c], precv.at[c], ps_s.at[c], ps_r.at[c], peer_id())

    def stat_send():
        return remote(stat_s, stat_r, st_s, st_r, peer_id())

    def ctx_send():
        return remote(ctx.at[pl.ds(0, tok)], ctx.at[pl.ds(tok, tok)], cx_s, cx_r, bit_id(0))

    def grad_peer(c):
        return remote(
            g.at[c, pl.ds(0, tok)], g.at[half + c, pl.ds(0, tok)], gy_s.at[c], gy_r.at[c], peer_id()
        )

    def grad_mate(r):
        return remote(
            g.at[r, pl.ds(0, tok)], g.at[r, pl.ds(tok, tok)], gm_s.at[r], gm_r.at[r], bit_id(0)
        )

    def shard_send(k, c):
        return remote(
            sends[k - 1].at[c], recvs[k - 1].at[c], rs_s.at[k - 1, c], rs_r.at[k - 1, c], bit_id(k)
        )

    def gain_send(b):
        device = bit_id(b) if b < bits else peer_id()
        return remote(gp.at[b], gpr.at[b], gg_s.at[b], gg_r.at[b], device)

    ctx_copy().start()

    @pl.loop(0, half)
    def _(c):
        w_copy(half + c).start()

    barrier = pltpu.get_barrier_semaphore()
    pl.semaphore_signal(barrier, inc=1, device_id=peer_id(), device_id_type=MESH)
    for bit in range(bits):
        pl.semaphore_signal(barrier, inc=1, device_id=bit_id(bit), device_id_type=MESH)
    pl.semaphore_wait(barrier, bits + 1)

    ctx_copy().wait()
    ctx_send().start()

    @pl.loop(0, half)
    def _(c):
        w_copy(c).start()
        cot_copy(c).start()

    gain_copy().start()

    @pl.loop(0, half)
    def _(c):
        w_copy(half + c).wait()
        psend[c] = jnp.dot(
            ctx[0:tok], wv[half + c], preferred_element_type=F32
        ).astype(BF16)
        partial_send(c).start()

    @pl.loop(0, half)
    def _(c):
        w_copy(c).wait()
        own[c] = jnp.dot(ctx[0:tok], wv[c], preferred_element_type=F32)
        cot_copy(c).wait()

    @pl.loop(0, chunks)
    def _(r):
        for copy in m_copies(r):
            copy.start()

    gain_copy().wait()
    for r in range(chunks):
        gain[r] = gain_flat[r * cw:(r + 1) * cw].reshape(1, cw)

    ctx_send().wait_recv()
    ctxt_all[...] = jnp.transpose(ctx[...].astype(F32)).reshape(n, rows, 2 * tok)
    blocks = []
    for place in range(n // 2):
        shard = dp
        for k in range(1, bits):
            if not (place >> (bits - 1 - k)) & 1:
                shard = flip(shard, k)
        blocks.append(ctxt_all[shard])
    ctxt[...] = jnp.concatenate(blocks, axis=0).astype(BF16)

    def fold(value):
        total = value[:, 0:128]
        for lane in range(128, cw, 128):
            total = total + value[:, lane:lane + 128]
        return total

    def gather_stats(c, carry):
        square, cross = carry
        partial_send(c).wait_recv()
        attn = own[c] + precv[c].astype(F32)
        own[c] = attn
        scaled = cot[c].astype(F32) * gain[mp * half + c]
        return square + fold(attn * attn), cross + fold(scaled * attn)

    zero = jnp.zeros((tok, 128), F32)
    square, cross = lax.fori_loop(0, half, gather_stats, (zero, zero))
    square = jnp.sum(square, axis=1, keepdims=True)
    cross = jnp.sum(cross, axis=1, keepdims=True)
    even = lax.broadcasted_iota(jnp.int32, (tok, 128), 1) % 2 == 0
    stat_s[...] = jnp.transpose(jnp.where(even, square, cross))[0:8]
    stat_send().start()
    stat_send().wait_recv()
    totals = jnp.transpose(jnp.concatenate([stat_s[...] + stat_r[...]] * 16, axis=0))
    inverse = lax.rsqrt(totals[:, 0:1] / width + norm_floor)
    shift = inverse * totals[:, 1:2] / width

    @pl.loop(0, half)
    def _(c):
        upstream = cot[c].astype(F32)
        normed = own[c] * inverse
        g[c, 0:tok] = (inverse * (upstream * gain[mp * half + c] - normed * shift)).astype(BF16)
        grad_peer(c).start()
        grad_mate(c).start()
        gp[0, c] = jnp.sum(upstream * normed, axis=0, keepdims=True)

    gc_acc[...] = jnp.zeros_like(gc_acc)
    gain_send(0).start()

    n_final = chunks + LAG * (bits - 1)

    @pl.loop(0, max(n_final, bits + 3))
    def _(t):
        ahead = t + AHEAD

        @pl.when((ahead >= half) & (ahead < chunks))
        def _():
            grad_peer(ahead - half).wait_recv()
            grad_mate(ahead).start()

        @pl.when(t < chunks)
        def _():
            grad_mate(t).wait_recv()
            product = jnp.dot(ctxt[...], g[t], preferred_element_type=F32)
            cut = product.shape[0] // 2
            sends[0][t] = product[:cut].astype(BF16)
            shard_send(1, t).start()
            keeps[0][t] = product[cut:]
            gc_acc[...] += lax.dot_general(
                g[t, 0:tok], wv[t], (((1,), (1,)), ((), ())), preferred_element_type=F32
            )

        @pl.when(t == chunks)
        def _():
            gc_out[...] = gc_acc[...].astype(BF16)

        for b in range(bits + 1):
            @pl.when(t == b + 1)
            def _():
                gain_send(b).wait_recv()
                if b < bits:
                    gp[b + 1] = gp[b] + gpr[b]
                    gain_send(b + 1).start()
                else:
                    gfin[pl.ds(mp * half, half)] = gp[bits]
                    gfin[pl.ds(peer * half, half)] = gpr[bits]

        for k in range(bits - 1, 0, -1):
            c = t - LAG * k

            @pl.when((c >= 0) & (c < chunks))
            def _():
                shard_send(k, c).wait_recv()
                total = keeps[k - 1][c] + recvs[k - 1][c].astype(F32)
                if k < bits - 1:
                    cut = total.shape[0] // 2
                    sends[k][c] = total[:cut].astype(BF16)
                    shard_send(k + 1, c).start()
                    keeps[k][c] = total[cut:]
                else:
                    for copy in m_copies(c):
                        copy.wait()
                    first = beta_one * m1[c] + (1.0 - beta_one) * total
                    second = beta_two * m2[c] + (1.0 - beta_two) * total * total
                    cols = pl.ds(column(c), cw)
                    nw[0, :, cols] = (
                        master[c].astype(F32) - learn_rate * first / (jnp.sqrt(second) + adam_floor)
                    ).astype(BF16)
                    n1[0, :, cols] = first
                    n2[0, :, cols] = second

    ctx_send().wait_send()
    stat_send().wait_send()

    @pl.loop(0, half)
    def _(c):
        partial_send(c).wait_send()
        grad_peer(c).wait_send()

    for b in range(bits + 1):
        gain_send(b).wait_send()

    @pl.loop(0, chunks)
    def _(r):
        grad_mate(r).wait_send()
        for k in range(1, bits):
            shard_send(k, r).wait_send()


def settle(nw, n1, n2, gg, gc, nw_out, n1_out, n2_out, gg_out, gc_out, flat, sem):
    pairs = ((nw, nw_out), (n1, n1_out), (n2, n2_out), (gc, gc_out))
    copies = [pltpu.make_async_copy(a, b, sem.at[i]) for i, (a, b) in enumerate(pairs)]
    for copy in copies:
        copy.start()
    chunks, _, cw = gg.shape
    for r in range(chunks):
        flat[r * cw:(r + 1) * cw] = gg[r].reshape(cw)
    copies.append(pltpu.make_async_copy(flat, gg_out, sem.at[4]))
    copies[-1].start()
    for copy in copies:
        copy.wait()


def per_device(n, context, out_weight, cotangent, norm_gain, first_moment, second_moment):
    tok, heads = context.shape
    width = out_weight.shape[1]
    rows = first_moment.shape[1]
    bits = n.bit_length() - 1
    cw = 256
    half = width // (2 * cw)
    chunks = 2 * half
    cfg = (n, bits, half, chunks, cw, rows, tok, heads, width)
    sizes = [(n >> (k + 1)) * rows for k in range(1, bits)]
    dma = pltpu.SemaphoreType.DMA
    vmem = pltpu.VMEM
    scratch = [
        vmem((chunks, heads, cw), BF16),
        vmem((2 * tok, heads), BF16),
        vmem((n, rows, 2 * tok), F32),
        vmem((heads // 2, 2 * tok), BF16),
        vmem((half, tok, cw), BF16),
        vmem((width,), F32),
        vmem((chunks, 1, cw), F32),
        vmem((half, tok, cw), BF16),
        vmem((half, tok, cw), BF16),
        vmem((half, tok, cw), F32),
        vmem((8, tok), F32),
        vmem((8, tok), F32),
        vmem((chunks, 2 * tok, cw), BF16),
        tuple(vmem((chunks, size, cw), BF16) for size in sizes),
        tuple(vmem((chunks, size, cw), BF16) for size in sizes),
        tuple(vmem((chunks, size, cw), F32) for size in sizes),
        vmem((chunks, rows, cw), F32),
        vmem((chunks, rows, cw), F32),
        vmem((chunks, rows, cw), BF16),
        vmem((tok, heads), F32),
        vmem((bits + 1, half, 1, cw), F32),
        vmem((bits + 1, half, 1, cw), F32),
        dma((2,)), dma((chunks,)), dma((half,)), dma((3, chunks)),
        dma((half,)), dma((half,)), dma, dma, dma, dma,
        dma((half,)), dma((half,)), dma((chunks,)), dma((chunks,)),
        dma((bits - 1, chunks)), dma((bits - 1, chunks)), dma((bits + 1,)), dma((bits + 1,)),
    ]
    anywhere = pl.BlockSpec(memory_space=pltpu.HBM)
    new_weight, new_first, new_second, grad_gain, grad_context = pl.pallas_call(
        functools.partial(kernel, cfg),
        out_shape=(
            jax.ShapeDtypeStruct(first_moment.shape, BF16),
            jax.ShapeDtypeStruct(first_moment.shape, F32),
            jax.ShapeDtypeStruct(first_moment.shape, F32),
            jax.ShapeDtypeStruct((chunks, 1, cw), F32),
            jax.ShapeDtypeStruct((tok, heads), BF16),
        ),
        in_specs=[anywhere] * 6,
        out_specs=(pl.BlockSpec(memory_space=pltpu.VMEM),) * 5,
        scratch_shapes=scratch,
        compiler_params=pltpu.CompilerParams(
            collective_id=0, has_side_effects=True, vmem_limit_bytes=50 * 1024 * 1024
        ),
    )(context, out_weight, cotangent, norm_gain, first_moment, second_moment)
    return pl.pallas_call(
        settle,
        out_shape=(
            jax.ShapeDtypeStruct(first_moment.shape, BF16),
            jax.ShapeDtypeStruct(first_moment.shape, F32),
            jax.ShapeDtypeStruct(first_moment.shape, F32),
            jax.ShapeDtypeStruct((width,), F32),
            jax.ShapeDtypeStruct((tok, heads), BF16),
        ),
        in_specs=[pl.BlockSpec(memory_space=pltpu.VMEM)] * 5,
        out_specs=(anywhere,) * 5,
        scratch_shapes=[vmem((width,), F32), dma((5,))],
        compiler_params=pltpu.CompilerParams(vmem_limit_bytes=8 * 1024 * 1024),
    )(new_weight, new_first, new_second, grad_gain, grad_context)


def solution(mesh):
    return jax.shard_map(
        functools.partial(per_device, mesh.shape["dp"]),
        mesh=mesh,
        in_specs=(
            P("dp", "mp"),
            P("mp", None),
            P("dp", None),
            P(),
            P("mp", "dp", None),
            P("mp", "dp", None),
        ),
        out_specs=(
            P("mp", "dp", None),
            P("mp", "dp", None),
            P("mp", "dp", None),
            P(),
            P("dp", "mp"),
        ),
        check_vma=False,
    )
```

profile of v0, /device:TPU:0, one launch (start us, length us, event | category | flops | bytes accessed | tf_op | source)
XLA Modules:
  0.0 96.2 jit_solution(6183800590936050956)
XLA Ops:
  0.6 0.0 copy-start
  0.6 1.1 %copy-done = bf16[320,1024]{1,0:T(8,128)(2,1)S(1)} copy-done((bf16[320,1024]{1,0:T(8,128)(2,1)S(1)}, bf16[320,1024]{1,0:T(8,128)(2,1)}, u32[]{:S(2)}) %copy-start) | copy-done | bytes 655384
  1.7 0.0 copy-start.1
  1.7 0.7 copy-done.1
  2.4 92.1 %shard_map.101 = (bf16[1,64,3584]{2,1,0:T(8,128)(2,1)S(1)}, f32[1,64,3584]{2,1,0:T(8,128)S(1)}, f32[1,64,3584]{2,1,0:T(8,128)S(1)}, f32[14,1,256]{2,1,0:T(1,128)S(1)}, bf16[320,1024]{1,0:T(8,128)(2,1)S(1)}) custom-call(bf16[320,1024]{1,0:T(8,128)(2,1)S(1)} %copy-done, bf16[1024,3584]{1,0:T(8,128)(2,1)} %w_hbm.1, bf16[320,3584]{1,0:T(8,128)(2,1)} %cot_hbm.1, ...), custom_call_target="tpu_custom_call" | custom-call | tf_op jit(solution)/shard_map/pallas_call | solution.py:336
  94.5 1.6 %shard_map.102 = (bf16[1,64,3584]{2,1,0:T(8,128)(2,1)}, f32[1,64,3584]{2,1,0:T(8,128)}, f32[1,64,3584]{2,1,0:T(8,128)}, f32[3584]{0:T(1024)}, bf16[320,1024]{1,0:T(8,128)(2,1)}) custom-call(bf16[1,64,3584]{2,1,0:T(8,128)(2,1)S(1)} %get-tuple-element.10.nw, f32[1,64,3584]{2,1,0:T(8,128)S(1)} %get-tuple-element.11.n1, ...), custom_call_target="tpu_custom_call" | custom-call | tf_op jit(solution)/shard_map/pallas_call | solution.py:352
Async XLA Ops:
  0.6 1.1 %copy-start = (bf16[320,1024]{1,0:T(8,128)(2,1)S(1)}, bf16[320,1024]{1,0:T(8,128)(2,1)}, u32[]{:S(2)}) copy-start(bf16[320,1024]{1,0:T(8,128)(2,1)} %ctx_hbm.1) | copy-start | bytes 1966084
  1.7 0.7 copy-start.1
where the time goes:
time: 96.4 us; the launch traced here: 96.2 us
  Pallas kernels  93.7 us (97%)
  local copies, waits for them, and re-layouts  1.8 us (2%)
    pallas_call x1, Pallas kernels, per_device(): pl.pallas_call(functools.partial(kernel, cfg), out_shape=(jax.ShapeDtypeS...  92.1 us

commit v1 on v0

v1 whole, which is shorter than its diff:
```python
import functools

import jax
import jax.numpy as jnp
from jax import lax
from jax.experimental import pallas as pl
from jax.experimental.pallas import tpu as pltpu
from jax.sharding import PartitionSpec as P

norm_floor = 0.1
learn_rate = 0.01
beta_one = 0.9
beta_two = 0.95
adam_floor = 1e-08

MESH = pl.DeviceIdType.MESH
F32 = jnp.float32
BF16 = jnp.bfloat16
VMEM_LIMIT = 50 * 1024 * 1024
LAG = 2
PRE = 5


def kernel(
    cfg,
    ctx_hbm, w_hbm, cot_hbm, gain_hbm, m1_hbm, m2_hbm,
    nw, n1, n2, gfin, gc_out,
    wv, ctx, ctxt_all, ctxt, cot, gain_flat, gain, psend, precv, own, stat_s, stat_r, g4, gx,
    sends, recvs, keeps, fsend, frecv, m1, m2, master, gc_acc,
    gp, gpr,
    in_sem, w_sem, cot_sem, m_sem,
    ps_s, ps_r, st_s, st_r, cx_s, cx_r, gy_s, gy_r, gx_s, gx_r, gm_s, gm_r, gr_s, gr_r,
    rs_s, rs_r, fx_s, fx_r, gg_s, gg_r,
):
    n, bits, quarter, cw, rows, tok, heads, width = cfg
    half = 2 * quarter
    chunks = 4 * quarter
    stages = bits - 2
    dp, mp = lax.axis_index("dp"), lax.axis_index("mp")
    peer = 1 - mp
    side = (dp // 2) % 2
    order = [*range(2, bits), 1]

    def flip(index, bit):
        return index + (1 << bit) * (1 - 2 * ((index // (1 << bit)) % 2))

    def peer_id():
        return (dp, peer)

    def bit_id(bit):
        return (flip(dp, bit), mp)

    def place(r):
        group = r // quarter
        across = group // 2
        x_side = side + across * (1 - 2 * side)
        y_half = mp + (group % 2) * (1 - 2 * mp)
        return (2 * y_half + x_side) * quarter + r % quarter

    def column(r):
        return pl.multiple_of(place(r) * cw, cw)

    def mine(h):
        return h + quarter * (h // quarter)

    def ctx_copy():
        return pltpu.make_async_copy(ctx_hbm, ctx.at[pl.ds(0, tok)], in_sem.at[0])

    def gain_copy():
        return pltpu.make_async_copy(gain_hbm, gain_flat, in_sem.at[1])

    def w_copy(r):
        return pltpu.make_async_copy(w_hbm.at[:, pl.ds(column(r), cw)], wv.at[r], w_sem.at[r])

    def cot_copy(h):
        return pltpu.make_async_copy(cot_hbm.at[:, pl.ds(column(mine(h)), cw)], cot.at[h], cot_sem.at[h])

    def m_copies():
        return (
            pltpu.make_async_copy(m1_hbm.at[0], m1, m_sem.at[0]),
            pltpu.make_async_copy(m2_hbm.at[0], m2, m_sem.at[1]),
            pltpu.make_async_copy(
                w_hbm.at[pl.ds(pl.multiple_of(dp * rows, rows), rows), :], master, m_sem.at[2]
            ),
        )

    def remote(src, dst, send_sem, recv_sem, device):
        return pltpu.make_async_remote_copy(
            src_ref=src, dst_ref=dst, send_sem=send_sem, recv_sem=recv_sem,
            device_id=device, device_id_type=MESH,
        )

    def partial_send(h):
        return remote(psend.at[h], precv.at[h], ps_s.at[h], ps_r.at[h], peer_id())

    def stat_send():
        return remote(stat_s, stat_r, st_s, st_r, peer_id())

    def ctx_send(a, b, i, bit):
        return remote(
            ctx.at[pl.ds(a * tok, tok)], ctx.at[pl.ds(b * tok, tok)], cx_s.at[i], cx_r.at[i], bit_id(bit)
        )

    def ctx_mate():
        return ctx_send(0, 1, 0, 0)

    def ctx_side():
        return ctx_send(0, 2, 1, 1)

    def ctx_relay():
        return ctx_send(2, 3, 2, 0)

    def grad_peer_near(j):
        return remote(
            g4.at[j, pl.ds(0, tok)], g4.at[quarter + j, pl.ds(0, tok)],
            gy_s.at[j], gy_r.at[j], peer_id(),
        )

    def grad_peer_far(j):
        return remote(
            gx.at[j], gx.at[quarter + j], gy_s.at[quarter + j], gy_r.at[quarter + j], peer_id()
        )

    def grad_side(i):
        return remote(gx.at[i], g4.at[i, pl.ds(2 * tok, tok)], gx_s.at[i], gx_r.at[i], bit_id(1))

    def grad_mate(i):
        return remote(
            g4.at[i, pl.ds(0, tok)], g4.at[i, pl.ds(tok, tok)], gm_s.at[i], gm_r.at[i], bit_id(0)
        )

    def grad_relay(i):
        return remote(
            g4.at[i, pl.ds(2 * tok, tok)], g4.at[i, pl.ds(3 * tok, tok)],
            gr_s.at[i], gr_r.at[i], bit_id(0),
        )

    def shard_send(s, i):
        return remote(
            sends[s].at[i], recvs[s].at[i], rs_s.at[s, i], rs_r.at[s, i], bit_id(order[s])
        )

    def swap_send(i):
        return remote(fsend.at[i], frecv.at[i], fx_s.at[i], fx_r.at[i], bit_id(1))

    steps = [0, *order]

    def gain_send(b):
        device = bit_id(steps[b]) if b < bits else peer_id()
        return remote(gp.at[b], gpr.at[b], gg_s.at[b], gg_r.at[b], device)

    ctx_copy().start()

    @pl.loop(0, quarter)
    def _(j):
        w_copy(quarter + j).start()
        w_copy(3 * quarter + j).start()

    barrier = pltpu.get_barrier_semaphore()
    pl.semaphore_signal(barrier, inc=1, device_id=peer_id(), device_id_type=MESH)
    for bit in range(bits):
        pl.semaphore_signal(barrier, inc=1, device_id=bit_id(bit), device_id_type=MESH)

    gain_copy().start()

    @pl.loop(0, quarter)
    def _(j):
        w_copy(j).start()
        w_copy(2 * quarter + j).start()
        cot_copy(j).start()
        cot_copy(quarter + j).start()

    for copy in m_copies():
        copy.start()

    def pair(near, far):
        w_copy(near).wait()
        w_copy(far).wait()
        return jnp.dot(
            ctx[0:tok], jnp.concatenate([wv[near], wv[far]], axis=1), preferred_element_type=F32
        )

    def partial(j):
        value = pair(quarter + j, 3 * quarter + j).astype(BF16)
        psend[j] = value[:, :cw]
        psend[quarter + j] = value[:, cw:]

    def partial_start(j):
        partial_send(j).start()
        partial_send(quarter + j).start()

    ctx_copy().wait()
    partial(0)
    pl.semaphore_wait(barrier, bits + 1)
    partial_start(0)
    ctx_side().start()
    ctx_mate().start()

    @pl.loop(1, quarter)
    def _(j):
        partial(j)
        partial_start(j)

    @pl.loop(0, quarter)
    def _(j):
        value = pair(j, 2 * quarter + j)
        own[j] = value[:, :cw]
        own[quarter + j] = value[:, cw:]

    gain_copy().wait()
    for r in range(chunks):
        gain[r] = gain_flat[r * cw:(r + 1) * cw].reshape(1, cw)

    def turn(p):
        ctxt_all[...] = jnp.transpose(
            ctx[2 * p * tok:2 * (p + 1) * tok].astype(F32)
        ).reshape(n, rows, 2 * tok)
        blocks = []
        for spot in range(n // 2):
            shard = dp
            for i, k in enumerate(order):
                if not (spot >> (bits - 2 - i)) & 1:
                    shard = flip(shard, k)
            blocks.append(ctxt_all[shard])
        ctxt[p] = jnp.concatenate(blocks, axis=0).astype(BF16)

    ctx_mate().wait_recv()
    turn(0)

    def gather_stats(h, carry):
        square, cross = carry
        cot_copy(h).wait()
        partial_send(h).wait_recv()
        attn = own[h] + precv[h].astype(F32)
        own[h] = attn
        scaled = cot[h].astype(F32) * gain[place(mine(h))]
        return square + attn * attn, cross + scaled * attn

    def gather_pair(j, carry):
        return gather_stats(quarter + j, gather_stats(j, carry))

    early, late = (2 * quarter) // 3, (5 * quarter) // 6
    zero = jnp.zeros((tok, cw), F32)
    carry = lax.fori_loop(0, early, gather_pair, (zero, zero))
    ctx_side().wait_recv()
    ctx_relay().start()
    carry = lax.fori_loop(early, late, gather_pair, carry)
    ctx_relay().wait_recv()
    turn(1)
    square, cross = lax.fori_loop(late, quarter, gather_pair, carry)
    square = jnp.sum(square, axis=1, keepdims=True)
    cross = jnp.sum(cross, axis=1, keepdims=True)
    even = lax.broadcasted_iota(jnp.int32, (tok, 128), 1) % 2 == 0
    stat_s[...] = jnp.transpose(jnp.where(even, square, cross))[0:8]
    stat_send().start()
    stat_send().wait_recv()
    totals = jnp.transpose(jnp.concatenate([stat_s[...] + stat_r[...]] * 16, axis=0))
    inverse = lax.rsqrt(totals[:, 0:1] / width + norm_floor)
    shift = inverse * totals[:, 1:2] / width

    def gradient(h):
        spot = place(mine(h))
        upstream = cot[h].astype(F32)
        normed = own[h] * inverse
        gp[0, spot - half * mp] = jnp.sum(upstream * normed, axis=0, keepdims=True)
        return (inverse * (upstream * gain[spot] - normed * shift)).astype(BF16)

    @pl.loop(0, quarter)
    def _(j):
        gx[j] = gradient(quarter + j)
        grad_side(j).start()
        grad_peer_far(j).start()
        g4[j, 0:tok] = gradient(j)
        grad_mate(j).start()

    @pl.loop(0, quarter)
    def _(j):
        grad_peer_near(j).start()

    gain_send(0).start()

    def context_part(u):
        left = jnp.concatenate([g4[u, 0:tok], gx[u]], axis=1)
        right = jnp.concatenate([wv[u], wv[half + u]], axis=1)
        return lax.dot_general(left, right, (((1,), (1,)), ((), ())), preferred_element_type=F32)

    gc_acc[...] = context_part(0)

    @pl.loop(1, PRE)
    def _(u):
        gc_acc[...] += context_part(u)

    def adam(total, r):
        cols = pl.ds(column(r), cw)
        first = beta_one * m1[:, cols] + (1.0 - beta_one) * total
        second = beta_two * m2[:, cols] + (1.0 - beta_two) * total * total
        nw[0, :, cols] = (
            master[:, cols].astype(F32) - learn_rate * first / (jnp.sqrt(second) + adam_floor)
        ).astype(BF16)
        n1[0, :, cols] = first
        n2[0, :, cols] = second

    for copy in m_copies():
        copy.wait()

    n_final = half + LAG * (stages + 1)

    @pl.loop(0, max(n_final, 3 * bits + 3))
    def _(t):
        @pl.when(t < quarter)
        def _():
            grad_peer_far(t).wait_recv()
            grad_side(quarter + t).start()

        @pl.when((t >= quarter) & (t < half))
        def _():
            grad_peer_near(t - quarter).wait_recv()
            grad_mate(t).start()

        @pl.when(t < half)
        def _():
            grad_side(t).wait_recv()
            grad_relay(t).start()

        unit = jnp.where(t < quarter, t + PRE, t)

        @pl.when((t < half) & ((t >= quarter) | (unit < quarter)))
        def _():
            gc_acc[...] += context_part(unit)

        @pl.when(t == half)
        def _():
            gc_out[...] = gc_acc[...].astype(BF16)

        for b in range(bits + 1):
            @pl.when(t == 3 * b + 1)
            def _():
                gain_send(b).wait_recv()
                if b < bits:
                    gp[b + 1] = gp[b] + gpr[b]
                    gain_send(b + 1).start()
                else:
                    gfin[pl.ds(mp * half, half)] = gp[bits]
                    gfin[pl.ds(peer * half, half)] = gpr[bits]

        late_swap = t - LAG * (stages + 1)

        @pl.when((late_swap >= 0) & (late_swap < half))
        def _():
            swap_send(late_swap).wait_recv()
            adam(frecv[late_swap].astype(F32), half + late_swap)

        for s in range(stages - 1, -1, -1):
            i = t - LAG * (s + 1)

            @pl.when((i >= 0) & (i < half))
            def _():
                shard_send(s, i).wait_recv()
                total = keeps[s][i] + recvs[s][i].astype(F32)
                cut = total.shape[0] // 2
                if s < stages - 1:
                    sends[s + 1][i] = total[:cut].astype(BF16)
                    shard_send(s + 1, i).start()
                    keeps[s + 1][i] = total[cut:]
                else:
                    fsend[i] = total[:cut].astype(BF16)
                    swap_send(i).start()
                    adam(total[cut:], i)

        @pl.when(t < half)
        def _():
            grad_mate(t).wait_recv()
            grad_relay(t).wait_recv()
            product = jnp.dot(ctxt[0], g4[t, 0:2 * tok], preferred_element_type=F32)
            product += jnp.dot(ctxt[1], g4[t, 2 * tok:4 * tok], preferred_element_type=F32)
            cut = product.shape[0] // 2
            sends[0][t] = product[:cut].astype(BF16)
            shard_send(0, t).start()
            keeps[0][t] = product[cut:]

    stat_send().wait_send()
    ctx_mate().wait_send()
    ctx_side().wait_send()
    ctx_relay().wait_send()

    @pl.loop(0, quarter)
    def _(j):
        grad_peer_near(j).wait_send()
        grad_peer_far(j).wait_send()

    for b in range(bits + 1):
        gain_send(b).wait_send()

    @pl.loop(0, half)
    def _(i):
        partial_send(i).wait_send()
        grad_side(i).wait_send()
        grad_mate(i).wait_send()
        grad_relay(i).wait_send()
        swap_send(i).wait_send()
        for s in range(stages):
            shard_send(s, i).wait_send()


def settle(nw, n1, n2, gg, gc, nw_out, n1_out, n2_out, gg_out, gc_out, flat, sem):
    pairs = ((nw, nw_out), (n1, n1_out), (n2, n2_out), (gc, gc_out))
    copies = [pltpu.make_async_copy(a, b, sem.at[i]) for i, (a, b) in enumerate(pairs)]
    for copy in copies:
        copy.start()
    chunks, _, cw = gg.shape
    for r in range(chunks):
        flat[r * cw:(r + 1) * cw] = gg[r].reshape(cw)
    copies.append(pltpu.make_async_copy(flat, gg_out, sem.at[4]))
    copies[-1].start()
    for copy in copies:
        copy.wait()


def per_device(n, context, out_weight, cotangent, norm_gain, first_moment, second_moment):
    tok, heads = context.shape
    width = out_weight.shape[1]
    rows = first_moment.shape[1]
    bits = n.bit_length() - 1
    cw = 128
    quarter = width // (4 * cw)
    half, chunks = 2 * quarter, 4 * quarter
    stages = bits - 2
    cfg = (n, bits, quarter, cw, rows, tok, heads, width)
    sizes = [(n >> (s + 2)) * rows for s in range(stages)]
    dma = pltpu.SemaphoreType.DMA
    vmem = pltpu.VMEM
    scratch = [
        vmem((chunks, heads, cw), BF16),
        vmem((4 * tok, heads), BF16),
        vmem((n, rows, 2 * tok), F32),
        vmem((2, heads // 2, 2 * tok), BF16),
        vmem((half, tok, cw), BF16),
        vmem((width,), F32),
        vmem((chunks, 1, cw), F32),
        vmem((half, tok, cw), BF16),
        vmem((half, tok, cw), BF16),
        vmem((half, tok, cw), F32),
        vmem((8, tok), F32),
        vmem((8, tok), F32),
        vmem((half, 4 * tok, cw), BF16),
        vmem((half, tok, cw), BF16),
        tuple(vmem((half, size, cw), BF16) for size in sizes),
        tuple(vmem((half, size, cw), BF16) for size in sizes),
        tuple(vmem((half, size, cw), F32) for size in sizes),
        vmem((half, rows, cw), BF16),
        vmem((half, rows, cw), BF16),
        vmem((rows, width), F32),
        vmem((rows, width), F32),
        vmem((rows, width), BF16),
        vmem((tok, heads), F32),
        vmem((bits + 1, half, 1, cw), F32),
        vmem((bits + 1, half, 1, cw), F32),
        dma((2,)), dma((chunks,)), dma((half,)), dma((3,)),
        dma((half,)), dma((half,)), dma, dma, dma((3,)), dma((3,)),
        dma((half,)), dma((half,)), dma((half,)), dma((half,)),
        dma((half,)), dma((half,)), dma((half,)), dma((half,)),
        dma((stages, half)), dma((stages, half)), dma((half,)), dma((half,)),
        dma((bits + 1,)), dma((bits + 1,)),
    ]
    anywhere = pl.BlockSpec(memory_space=pltpu.HBM)
    new_weight, new_first, new_second, grad_gain, grad_context = pl.pallas_call(
        functools.partial(kernel, cfg),
        out_shape=(
            jax.ShapeDtypeStruct(first_moment.shape, BF16),
            jax.ShapeDtypeStruct(first_moment.shape, F32),
            jax.ShapeDtypeStruct(first_moment.shape, F32),
            jax.ShapeDtypeStruct((chunks, 1, cw), F32),
            jax.ShapeDtypeStruct((tok, heads), BF16),
        ),
        in_specs=[anywhere] * 6,
        out_specs=(pl.BlockSpec(memory_space=pltpu.VMEM),) * 5,
        scratch_shapes=scratch,
        compiler_params=pltpu.CompilerParams(
            collective_id=0, has_side_effects=True, vmem_limit_bytes=VMEM_LIMIT
        ),
    )(context, out_weight, cotangent, norm_gain, first_moment, second_moment)
    return pl.pallas_call(
        settle,
        out_shape=(
            jax.ShapeDtypeStruct(first_moment.shape, BF16),
            jax.ShapeDtypeStruct(first_moment.shape, F32),
            jax.ShapeDtypeStruct(first_moment.shape, F32),
            jax.ShapeDtypeStruct((width,), F32),
            jax.ShapeDtypeStruct((tok, heads), BF16),
        ),
        in_specs=[pl.BlockSpec(memory_space=pltpu.VMEM)] * 5,
        out_specs=(anywhere,) * 5,
        scratch_shapes=[vmem((width,), F32), dma((5,))],
        compiler_params=pltpu.CompilerParams(vmem_limit_bytes=8 * 1024 * 1024),
    )(new_weight, new_first, new_second, grad_gain, grad_context)


def solution(mesh):
    return jax.shard_map(
        functools.partial(per_device, mesh.shape["dp"]),
        mesh=mesh,
        in_specs=(
            P("dp", "mp"),
            P("mp", None),
            P("dp", None),
            P(),
            P("mp", "dp", None),
            P("mp", "dp", None),
        ),
        out_specs=(
            P("mp", "dp", None),
            P("mp", "dp", None),
            P("mp", "dp", None),
            P(),
            P("dp", "mp"),
        ),
        check_vma=False,
    )
```

time: 96.4 us -> 90.3 us (0.937)
  Pallas kernels: 93.7 us -> 87.6 us
    pallas_call x1, Pallas kernels: 92.1 us -> 86 us  [per_device(): pl.pallas_call(functools.partial(kernel, cfg), out_shape=(jax.ShapeDtypeS...]
where the time goes in v1:
time: 90.3 us; the launch traced here: 90 us
  Pallas kernels  87.6 us (97%)
  local copies, waits for them, and re-layouts  1.8 us (2%)
    pallas_call x1, Pallas kernels, per_device(): pl.pallas_call(functools.partial(kernel, cfg), out_shape=(jax.ShapeDtypeS...  86 us

profile of v1, /device:TPU:0, one launch (start us, length us, event | category | flops | bytes accessed | tf_op | source)
XLA Modules:
  0.0 90.0 jit_solution(3534209619090299513)
XLA Ops:
  0.6 0.0 copy-start
  0.6 1.1 %copy-done = bf16[320,1024]{1,0:T(8,128)(2,1)S(1)} copy-done((bf16[320,1024]{1,0:T(8,128)(2,1)S(1)}, bf16[320,1024]{1,0:T(8,128)(2,1)}, u32[]{:S(2)}) %copy-start) | copy-done | bytes 655384
  1.7 0.0 copy-start.1
  1.7 0.7 copy-done.1
  2.4 86.0 %shard_map.101 = (bf16[1,64,3584]{2,1,0:T(8,128)(2,1)S(1)}, f32[1,64,3584]{2,1,0:T(8,128)S(1)}, f32[1,64,3584]{2,1,0:T(8,128)S(1)}, f32[28,1,128]{2,1,0:T(1,128)S(1)}, bf16[320,1024]{1,0:T(8,128)(2,1)S(1)}) custom-call(bf16[320,1024]{1,0:T(8,128)(2,1)S(1)} %copy-done, bf16[1024,3584]{1,0:T(8,128)(2,1)} %w_hbm.1, bf16[320,3584]{1,0:T(8,128)(2,1)} %cot_hbm.1, ...), custom_call_target="tpu_custom_call" | custom-call | tf_op jit(solution)/shard_map/pallas_call | solution.py:466
  88.4 1.6 %shard_map.102 = (bf16[1,64,3584]{2,1,0:T(8,128)(2,1)}, f32[1,64,3584]{2,1,0:T(8,128)}, f32[1,64,3584]{2,1,0:T(8,128)}, f32[3584]{0:T(1024)}, bf16[320,1024]{1,0:T(8,128)(2,1)}) custom-call(bf16[1,64,3584]{2,1,0:T(8,128)(2,1)S(1)} %get-tuple-element.10.nw, f32[1,64,3584]{2,1,0:T(8,128)S(1)} %get-tuple-element.11.n1, ...), custom_call_target="tpu_custom_call" | custom-call | tf_op jit(solution)/shard_map/pallas_call | solution.py:482
Async XLA Ops:
  0.6 1.1 %copy-start = (bf16[320,1024]{1,0:T(8,128)(2,1)S(1)}, bf16[320,1024]{1,0:T(8,128)(2,1)}, u32[]{:S(2)}) copy-start(bf16[320,1024]{1,0:T(8,128)(2,1)} %ctx_hbm.1) | copy-start | bytes 1966084
  1.7 0.7 copy-start.1

commit v2 on v1

--- a/solution.py
+++ b/solution.py
@@ -18,14 +18,14 @@
 BF16 = jnp.bfloat16
 VMEM_LIMIT = 50 * 1024 * 1024
 LAG = 2
-PRE = 5
+SWAP = 8
 
 
 def kernel(
     cfg,
     ctx_hbm, w_hbm, cot_hbm, gain_hbm, m1_hbm, m2_hbm,
     nw, n1, n2, gfin, gc_out,
-    wv, ctx, ctxt_all, ctxt, cot, gain_flat, gain, psend, precv, own, stat_s, stat_r, g4, gx,
+    wv, ctx, ctxt_all, ctxt, cot, gain_flat, gain, psend, precv, own, stat_s, stat_r, inverse_v, shift_v, g4, gx,
     sends, recvs, keeps, fsend, frecv, m1, m2, master, gc_acc,
     gp, gpr,
     in_sem, w_sem, cot_sem, m_sem,
@@ -50,18 +50,18 @@
     def bit_id(bit):
         return (flip(dp, bit), mp)
 
-    def place(r):
-        group = r // quarter
-        across = group // 2
-        x_side = side + across * (1 - 2 * side)
-        y_half = mp + (group % 2) * (1 - 2 * mp)
-        return (2 * y_half + x_side) * quarter + r % quarter
-
-    def column(r):
-        return pl.multiple_of(place(r) * cw, cw)
-
-    def mine(h):
-        return h + quarter * (h // quarter)
+    starts = [
+        (2 * y_half + x_side) * quarter
+        for x_side in (side, 1 - side) for y_half in (mp, peer)
+    ]
+
+    def cols(group, j):
+        return pl.ds(pl.multiple_of((starts[group] + j) * cw, cw), cw)
+
+    def cols_of(across, i):
+        near, far = starts[2 * across:2 * across + 2]
+        first = jnp.where(i < quarter, near + i, far + i - quarter)
+        return pl.ds(pl.multiple_of(first * cw, cw), cw)
 
     def ctx_copy():
         return pltpu.make_async_copy(ctx_hbm, ctx.at[pl.ds(0, tok)], in_sem.at[0])
@@ -69,11 +69,13 @@
     def gain_copy():
         return pltpu.make_async_copy(gain_hbm, gain_flat, in_sem.at[1])
 
-    def w_copy(r):
-        return pltpu.make_async_copy(w_hbm.at[:, pl.ds(column(r), cw)], wv.at[r], w_sem.at[r])
-
-    def cot_copy(h):
-        return pltpu.make_async_copy(cot_hbm.at[:, pl.ds(column(mine(h)), cw)], cot.at[h], cot_sem.at[h])
+    def w_copy(group, j):
+        r = group * quarter + j
+        return pltpu.make_async_copy(w_hbm.at[:, cols(group, j)], wv.at[r], w_sem.at[r])
+
+    def cot_copy(far, j):
+        h = far * quarter + j
+        return pltpu.make_async_copy(cot_hbm.at[:, cols(2 * far, j)], cot.at[h], cot_sem.at[h])
 
     def m_copies():
         return (
@@ -149,39 +151,26 @@
         device = bit_id(steps[b]) if b < bits else peer_id()
         return remote(gp.at[b], gpr.at[b], gg_s.at[b], gg_r.at[b], device)
 
+    barrier = pltpu.get_barrier_semaphore()
+    pl.semaphore_signal(barrier, inc=1, device_id=peer_id(), device_id_type=MESH)
+    for bit in range(bits - 1, -1, -1):
+        pl.semaphore_signal(barrier, inc=1, device_id=bit_id(bit), device_id_type=MESH)
+
     ctx_copy().start()
 
     @pl.loop(0, quarter)
     def _(j):
-        w_copy(quarter + j).start()
-        w_copy(3 * quarter + j).start()
-
-    barrier = pltpu.get_barrier_semaphore()
-    pl.semaphore_signal(barrier, inc=1, device_id=peer_id(), device_id_type=MESH)
-    for bit in range(bits):
-        pl.semaphore_signal(barrier, inc=1, device_id=bit_id(bit), device_id_type=MESH)
-
-    gain_copy().start()
-
-    @pl.loop(0, quarter)
-    def _(j):
-        w_copy(j).start()
-        w_copy(2 * quarter + j).start()
-        cot_copy(j).start()
-        cot_copy(quarter + j).start()
-
-    for copy in m_copies():
-        copy.start()
-
-    def pair(near, far):
-        w_copy(near).wait()
-        w_copy(far).wait()
-        return jnp.dot(
-            ctx[0:tok], jnp.concatenate([wv[near], wv[far]], axis=1), preferred_element_type=F32
-        )
+        w_copy(1, j).start()
+        w_copy(3, j).start()
+
+    def pair(near, far, j):
+        w_copy(near, j).wait()
+        w_copy(far, j).wait()
+        right = jnp.concatenate([wv[near * quarter + j], wv[far * quarter + j]], axis=1)
+        return jnp.dot(ctx[0:tok], right, preferred_element_type=F32)
 
     def partial(j):
-        value = pair(quarter + j, 3 * quarter + j).astype(BF16)
+        value = pair(1, 3, j).astype(BF16)
         psend[j] = value[:, :cw]
         psend[quarter + j] = value[:, cw:]
 
@@ -200,12 +189,25 @@
     def _(j):
         partial(j)
         partial_start(j)
-
-    @pl.loop(0, quarter)
-    def _(j):
-        value = pair(j, 2 * quarter + j)
+        w_copy(0, j).start()
+        w_copy(2, j).start()
+        cot_copy(0, j).start()
+        cot_copy(1, j).start()
+
+    for group in (0, 2):
+        w_copy(group, 0).start()
+        cot_copy(group // 2, 0).start()
+    gain_copy().start()
+
+    @pl.loop(1, quarter + 1)
+    def _(k):
+        j = jnp.where(k == quarter, 0, k)
+        value = pair(0, 2, j)
         own[j] = value[:, :cw]
         own[quarter + j] = value[:, cw:]
+
+    for copy in m_copies():
+        copy.start()
 
     gain_copy().wait()
     for r in range(chunks):
@@ -227,17 +229,18 @@
     ctx_mate().wait_recv()
     turn(0)
 
-    def gather_stats(h, carry):
+    def gather_stats(far, j, carry):
         square, cross = carry
-        cot_copy(h).wait()
+        h = far * quarter + j
+        cot_copy(far, j).wait()
         partial_send(h).wait_recv()
         attn = own[h] + precv[h].astype(F32)
         own[h] = attn
-        scaled = cot[h].astype(F32) * gain[place(mine(h))]
+        scaled = cot[h].astype(F32) * gain[starts[2 * far] + j]
         return square + attn * attn, cross + scaled * attn
 
     def gather_pair(j, carry):
-        return gather_stats(quarter + j, gather_stats(j, carry))
+        return gather_stats(1, j, gather_stats(0, j, carry))
 
     early, late = (2 * quarter) // 3, (5 * quarter) // 6
     zero = jnp.zeros((tok, cw), F32)
@@ -254,27 +257,34 @@
     stat_s[...] = jnp.transpose(jnp.where(even, square, cross))[0:8]
     stat_send().start()
     stat_send().wait_recv()
-    totals = jnp.transpose(jnp.concatenate([stat_s[...] + stat_r[...]] * 16, axis=0))
-    inverse = lax.rsqrt(totals[:, 0:1] / width + norm_floor)
-    shift = inverse * totals[:, 1:2] / width
-
-    def gradient(h):
-        spot = place(mine(h))
+    totals = stat_s[...] + stat_r[...]
+
+    def spread(row):
+        return jnp.transpose(jnp.concatenate([totals[row:row + 1]] * 128, axis=0))
+
+    inverse = lax.rsqrt(spread(0) / width + norm_floor)
+    inverse_v[...] = inverse
+    shift_v[...] = inverse * spread(1) / width
+
+    def gradient(far, j):
+        h = far * quarter + j
+        spot = starts[2 * far] + j
+        inverse = inverse_v[...]
         upstream = cot[h].astype(F32)
         normed = own[h] * inverse
         gp[0, spot - half * mp] = jnp.sum(upstream * normed, axis=0, keepdims=True)
-        return (inverse * (upstream * gain[spot] - normed * shift)).astype(BF16)
+        return (inverse * (upstream * gain[spot] - normed * shift_v[...])).astype(BF16)
 
     @pl.loop(0, quarter)
     def _(j):
-        gx[j] = gradient(quarter + j)
+        gx[j] = gradient(1, j)
         grad_side(j).start()
         grad_peer_far(j).start()
-        g4[j, 0:tok] = gradient(j)
-        grad_mate(j).start()
 
     @pl.loop(0, quarter)
     def _(j):
+        g4[j, 0:tok] = gradient(0, j)
+        grad_mate(j).start()
         grad_peer_near(j).start()
 
     gain_send(0).start()
@@ -286,12 +296,11 @@
 
     gc_acc[...] = context_part(0)
 
-    @pl.loop(1, PRE)
+    @pl.loop(1, quarter)
     def _(u):
         gc_acc[...] += context_part(u)
 
-    def adam(total, r):
-        cols = pl.ds(column(r), cw)
+    def adam(total, cols):
         first = beta_one * m1[:, cols] + (1.0 - beta_one) * total
         second = beta_two * m2[:, cols] + (1.0 - beta_two) * total * total
         nw[0, :, cols] = (
@@ -303,30 +312,20 @@
     for copy in m_copies():
         copy.wait()
 
-    n_final = half + LAG * (stages + 1)
-
-    @pl.loop(0, max(n_final, 3 * bits + 3))
+    swap_lag = LAG * stages + SWAP
+
+    @pl.loop(0, max(half + swap_lag, 3 * bits + 3))
     def _(t):
-        @pl.when(t < quarter)
+        @pl.when(t < half)
         def _():
-            grad_peer_far(t).wait_recv()
-            grad_side(quarter + t).start()
+            grad_side(t).wait_recv()
+            grad_relay(t).start()
 
         @pl.when((t >= quarter) & (t < half))
         def _():
             grad_peer_near(t - quarter).wait_recv()
             grad_mate(t).start()
-
-        @pl.when(t < half)
-        def _():
-            grad_side(t).wait_recv()
-            grad_relay(t).start()
-
-        unit = jnp.where(t < quarter, t + PRE, t)
-
-        @pl.when((t < half) & ((t >= quarter) | (unit < quarter)))
-        def _():
-            gc_acc[...] += context_part(unit)
+            gc_acc[...] += context_part(t)
 
         @pl.when(t == half)
         def _():
@@ -343,12 +342,12 @@
                     gfin[pl.ds(mp * half, half)] = gp[bits]
                     gfin[pl.ds(peer * half, half)] = gpr[bits]
 
-        late_swap = t - LAG * (stages + 1)
+        late_swap = t - swap_lag
 
         @pl.when((late_swap >= 0) & (late_swap < half))
         def _():
             swap_send(late_swap).wait_recv()
-            adam(frecv[late_swap].astype(F32), half + late_swap)
+            adam(frecv[late_swap].astype(F32), cols_of(1, late_swap))
 
         for s in range(stages - 1, -1, -1):
             i = t - LAG * (s + 1)
@@ -365,7 +364,7 @@
                 else:
                     fsend[i] = total[:cut].astype(BF16)
                     swap_send(i).start()
-                    adam(total[cut:], i)
+                    adam(total[cut:], cols_of(0, i))
 
         @pl.when(t < half)
         def _():
@@ -377,6 +376,11 @@
             sends[0][t] = product[:cut].astype(BF16)
             shard_send(0, t).start()
             keeps[0][t] = product[cut:]
+
+        @pl.when(t < quarter)
+        def _():
+            grad_peer_far(t).wait_recv()
+            grad_side(quarter + t).start()
 
     stat_send().wait_send()
     ctx_mate().wait_send()
@@ -442,6 +446,8 @@
         vmem((half, tok, cw), F32),
         vmem((8, tok), F32),
         vmem((8, tok), F32),
+        vmem((tok, cw), F32),
+        vmem((tok, cw), F32),
         vmem((half, 4 * tok, cw), BF16),
         vmem((half, tok, cw), BF16),
         tuple(vmem((half, size, cw), BF16) for size in sizes),
@@ -463,6 +469,7 @@
         dma((bits + 1,)), dma((bits + 1,)),
     ]
     anywhere = pl.BlockSpec(memory_space=pltpu.HBM)
+    pin = functools.partial(pltpu.with_memory_space_constraint, memory_space=pltpu.HBM)
     new_weight, new_first, new_second, grad_gain, grad_context = pl.pallas_call(
         functools.partial(kernel, cfg),
         out_shape=(
@@ -478,7 +485,7 @@
         compiler_params=pltpu.CompilerParams(
             collective_id=0, has_side_effects=True, vmem_limit_bytes=VMEM_LIMIT
         ),
-    )(context, out_weight, cotangent, norm_gain, first_moment, second_moment)
+    )(*map(pin, (context, out_weight, cotangent, norm_gain, first_moment, second_moment)))
     return pl.pallas_call(
         settle,
         out_shape=(

time: 90.3 us -> 83.3 us (0.922)
  Pallas kernels: 87.6 us -> 82.5 us
  local copies, waits for them, and re-layouts: 1.8 us -> 0 us
    pallas_call x1, Pallas kernels: 86 us -> 80.8 us  [per_device(): pl.pallas_call(functools.partial(kernel, cfg), out_shape=(jax.ShapeDtypeS...]
    unnamed x4 -> x0, local copies, waits for them, and re-layouts: 1.8 us -> none
where the time goes in v2:
time: 83.3 us; the launch traced here: 83.1 us
  Pallas kernels  82.5 us (99%)
    pallas_call x1, Pallas kernels, per_device(): pl.pallas_call(functools.partial(kernel, cfg), out_shape=(jax.ShapeDtypeS...  80.8 us

profile of v2, /device:TPU:0, one launch (start us, length us, event | category | flops | bytes accessed | tf_op | source)
XLA Modules:
  0.0 83.1 jit_solution(11853051385846589985)
XLA Ops:
  0.6 80.8 %shard_map.101 = (bf16[1,64,3584]{2,1,0:T(8,128)(2,1)S(1)}, f32[1,64,3584]{2,1,0:T(8,128)S(1)}, f32[1,64,3584]{2,1,0:T(8,128)S(1)}, f32[28,1,128]{2,1,0:T(1,128)S(1)}, bf16[320,1024]{1,0:T(8,128)(2,1)S(1)}) custom-call(bf16[320,1024]{1,0:T(8,128)(2,1)} %ctx_hbm.1, bf16[1024,3584]{1,0:T(8,128)(2,1)} %w_hbm.1, bf16[320,3584]{1,0:T(8,128)(2,1)} %cot_hbm.1, ...), custom_call_target="tpu_custom_call" | custom-call | tf_op jit(solution)/shard_map/pallas_call | solution.py:473
  81.5 1.6 %shard_map.102 = (bf16[1,64,3584]{2,1,0:T(8,128)(2,1)}, f32[1,64,3584]{2,1,0:T(8,128)}, f32[1,64,3584]{2,1,0:T(8,128)}, f32[3584]{0:T(1024)}, bf16[320,1024]{1,0:T(8,128)(2,1)}) custom-call(bf16[1,64,3584]{2,1,0:T(8,128)(2,1)S(1)} %get-tuple-element.10.nw, f32[1,64,3584]{2,1,0:T(8,128)S(1)} %get-tuple-element.11.n1, ...), custom_call_target="tpu_custom_call" | custom-call | tf_op jit(solution)/shard_map/pallas_call | solution.py:489

commit v3 on v2

--- a/solution.py
+++ b/solution.py
@@ -17,8 +17,9 @@
 F32 = jnp.float32
 BF16 = jnp.bfloat16
 VMEM_LIMIT = 50 * 1024 * 1024
-LAG = 2
-SWAP = 8
+LAG = 3
+SWAP = 6
+FIRST = 2
 
 
 def kernel(
@@ -29,7 +30,7 @@
     sends, recvs, keeps, fsend, frecv, m1, m2, master, gc_acc,
     gp, gpr,
     in_sem, w_sem, cot_sem, m_sem,
-    ps_s, ps_r, st_s, st_r, cx_s, cx_r, gy_s, gy_r, gx_s, gx_r, gm_s, gm_r, gr_s, gr_r,
+    ps_s, ps_r, st_s, st_r, cx_s, cx_r, gy_s, gy_r, gx_s, gx_r, gm_s, gm_r,
     rs_s, rs_r, fx_s, fx_r, gg_s, gg_r,
 ):
     n, bits, quarter, cw, rows, tok, heads, width = cfg
@@ -69,13 +70,19 @@
     def gain_copy():
         return pltpu.make_async_copy(gain_hbm, gain_flat, in_sem.at[1])
 
-    def w_copy(group, j):
-        r = group * quarter + j
-        return pltpu.make_async_copy(w_hbm.at[:, cols(group, j)], wv.at[r], w_sem.at[r])
+    def w_copy(group, j, sem):
+        base = half * (1 - group % 2)
+        return pltpu.make_async_copy(
+            w_hbm.at[:, cols(group, j)], wv.at[base + 2 * j + group // 2], sem
+        )
+
+    def w_wait(first, last, sem):
+        block = wv.at[pl.ds(first, last - first)]
+        pltpu.make_async_copy(block, block, sem).wait()
 
     def cot_copy(far, j):
         h = far * quarter + j
-        return pltpu.make_async_copy(cot_hbm.at[:, cols(2 * far, j)], cot.at[h], cot_sem.at[h])
+        return pltpu.make_async_copy(cot_hbm.at[:, cols(2 * far, j)], cot.at[h], cot_sem)
 
     def m_copies():
         return (
@@ -93,14 +100,14 @@
         )
 
     def partial_send(h):
-        return remote(psend.at[h], precv.at[h], ps_s.at[h], ps_r.at[h], peer_id())
+        return remote(psend.at[h], precv.at[h], ps_s, ps_r.at[h], peer_id())
 
     def stat_send():
         return remote(stat_s, stat_r, st_s, st_r, peer_id())
 
     def ctx_send(a, b, i, bit):
         return remote(
-            ctx.at[pl.ds(a * tok, tok)], ctx.at[pl.ds(b * tok, tok)], cx_s.at[i], cx_r.at[i], bit_id(bit)
+            ctx.at[pl.ds(a * tok, tok)], ctx.at[pl.ds(b * tok, tok)], cx_s, cx_r.at[i], bit_id(bit)
         )
 
     def ctx_mate():
@@ -115,41 +122,45 @@
     def grad_peer_near(j):
         return remote(
             g4.at[j, pl.ds(0, tok)], g4.at[quarter + j, pl.ds(0, tok)],
-            gy_s.at[j], gy_r.at[j], peer_id(),
+            gy_s.at[0], gy_r.at[j], peer_id(),
         )
 
     def grad_peer_far(j):
         return remote(
-            gx.at[j], gx.at[quarter + j], gy_s.at[quarter + j], gy_r.at[quarter + j], peer_id()
+            gx.at[j], gx.at[quarter + j], gy_s.at[1], gy_r.at[quarter + j], peer_id()
         )
 
     def grad_side(i):
-        return remote(gx.at[i], g4.at[i, pl.ds(2 * tok, tok)], gx_s.at[i], gx_r.at[i], bit_id(1))
+        return remote(gx.at[i], g4.at[i, pl.ds(2 * tok, tok)], gx_s, gx_r.at[i], bit_id(1))
 
     def grad_mate(i):
         return remote(
-            g4.at[i, pl.ds(0, tok)], g4.at[i, pl.ds(tok, tok)], gm_s.at[i], gm_r.at[i], bit_id(0)
+            g4.at[i, pl.ds(0, tok)], g4.at[i, pl.ds(tok, tok)], gm_s.at[0], gm_r.at[i], bit_id(0)
         )
 
     def grad_relay(i):
         return remote(
             g4.at[i, pl.ds(2 * tok, tok)], g4.at[i, pl.ds(3 * tok, tok)],
-            gr_s.at[i], gr_r.at[i], bit_id(0),
-        )
+            gm_s.at[1], gm_r.at[i], bit_id(0),
+        )
+
+    def grad_chip(i):
+        both = g4.at[i, pl.ds(0, 2 * tok)]
+        return remote(both, both, gm_s.at[0], gm_r.at[i], bit_id(0))
 
     def shard_send(s, i):
         return remote(
-            sends[s].at[i], recvs[s].at[i], rs_s.at[s, i], rs_r.at[s, i], bit_id(order[s])
+            sends[s].at[i], recvs[s].at[i], rs_s.at[s], rs_r.at[s, i], bit_id(order[s])
         )
 
     def swap_send(i):
-        return remote(fsend.at[i], frecv.at[i], fx_s.at[i], fx_r.at[i], bit_id(1))
+        return remote(fsend.at[i], frecv.at[i], fx_s, fx_r.at[i], bit_id(1))
 
     steps = [0, *order]
 
     def gain_send(b):
         device = bit_id(steps[b]) if b < bits else peer_id()
-        return remote(gp.at[b], gpr.at[b], gg_s.at[b], gg_r.at[b], device)
+        return remote(gp.at[b], gpr.at[b], gg_s, gg_r.at[b], device)
 
     barrier = pltpu.get_barrier_semaphore()
     pl.semaphore_signal(barrier, inc=1, device_id=peer_id(), device_id_type=MESH)
@@ -157,20 +168,15 @@
         pl.semaphore_signal(barrier, inc=1, device_id=bit_id(bit), device_id_type=MESH)
 
     ctx_copy().start()
-
-    @pl.loop(0, quarter)
-    def _(j):
-        w_copy(1, j).start()
-        w_copy(3, j).start()
-
-    def pair(near, far, j):
-        w_copy(near, j).wait()
-        w_copy(far, j).wait()
-        right = jnp.concatenate([wv[near * quarter + j], wv[far * quarter + j]], axis=1)
+    w_copy(1, 0, w_sem.at[0]).start()
+    w_copy(3, 0, w_sem.at[0]).start()
+
+    def pair(base, j):
+        right = jnp.concatenate([wv[base + 2 * j], wv[base + 2 * j + 1]], axis=1)
         return jnp.dot(ctx[0:tok], right, preferred_element_type=F32)
 
     def partial(j):
-        value = pair(1, 3, j).astype(BF16)
+        value = pair(0, j).astype(BF16)
         psend[j] = value[:, :cw]
         psend[quarter + j] = value[:, cw:]
 
@@ -179,30 +185,41 @@
         partial_send(quarter + j).start()
 
     ctx_copy().wait()
+    w_wait(0, 2, w_sem.at[0])
+
+    @pl.loop(1, quarter)
+    def _(j):
+        w_copy(1, j, w_sem.at[1]).start()
+        w_copy(3, j, w_sem.at[1]).start()
+
+    @pl.loop(0, quarter)
+    def _(j):
+        w_copy(0, j, w_sem.at[2]).start()
+        w_copy(2, j, w_sem.at[2]).start()
+
     partial(0)
     pl.semaphore_wait(barrier, bits + 1)
+
     partial_start(0)
+    w_wait(2, half, w_sem.at[1])
+
+    @pl.loop(1, quarter)
+    def _(j):
+        partial(j)
+        partial_start(j)
+        cot_copy(0, j).start()
+        cot_copy(1, j).start()
+
     ctx_side().start()
     ctx_mate().start()
-
-    @pl.loop(1, quarter)
-    def _(j):
-        partial(j)
-        partial_start(j)
-        w_copy(0, j).start()
-        w_copy(2, j).start()
-        cot_copy(0, j).start()
-        cot_copy(1, j).start()
-
-    for group in (0, 2):
-        w_copy(group, 0).start()
-        cot_copy(group // 2, 0).start()
+    cot_copy(0, 0).start()
+    cot_copy(1, 0).start()
     gain_copy().start()
-
-    @pl.loop(1, quarter + 1)
-    def _(k):
-        j = jnp.where(k == quarter, 0, k)
-        value = pair(0, 2, j)
+    w_wait(half, chunks, w_sem.at[2])
+
+    @pl.loop(0, quarter)
+    def _(j):
+        value = pair(half, j)
         own[j] = value[:, :cw]
         own[quarter + j] = value[:, cw:]
 
@@ -226,13 +243,13 @@
             blocks.append(ctxt_all[shard])
         ctxt[p] = jnp.concatenate(blocks, axis=0).astype(BF16)
 
+    pltpu.make_async_copy(cot, cot, cot_sem).wait()
     ctx_mate().wait_recv()
     turn(0)
 
     def gather_stats(far, j, carry):
         square, cross = carry
         h = far * quarter + j
-        cot_copy(far, j).wait()
         partial_send(h).wait_recv()
         attn = own[h] + precv[h].astype(F32)
         own[h] = attn
@@ -275,30 +292,40 @@
         gp[0, spot - half * mp] = jnp.sum(upstream * normed, axis=0, keepdims=True)
         return (inverse * (upstream * gain[spot] - normed * shift_v[...])).astype(BF16)
 
-    @pl.loop(0, quarter)
-    def _(j):
+    def far_part(j):
         gx[j] = gradient(1, j)
         grad_side(j).start()
         grad_peer_far(j).start()
 
+    @pl.loop(0, FIRST)
+    def _(j):
+        far_part(j)
+
     @pl.loop(0, quarter)
     def _(j):
         g4[j, 0:tok] = gradient(0, j)
         grad_mate(j).start()
+
+    def context_part(u, base):
+        left = jnp.concatenate([g4[u, 0:tok], gx[u]], axis=1)
+        right = jnp.concatenate([wv[base], wv[base + 1]], axis=1)
+        return lax.dot_general(left, right, (((1,), (1,)), ((), ())), preferred_element_type=F32)
+
+    gc_acc[...] = context_part(0, half)
+
+    @pl.loop(FIRST, quarter)
+    def _(j):
+        far_part(j)
+
+    gain_send(0).start()
+
+    @pl.loop(0, quarter)
+    def _(j):
         grad_peer_near(j).start()
-
-    gain_send(0).start()
-
-    def context_part(u):
-        left = jnp.concatenate([g4[u, 0:tok], gx[u]], axis=1)
-        right = jnp.concatenate([wv[u], wv[half + u]], axis=1)
-        return lax.dot_general(left, right, (((1,), (1,)), ((), ())), preferred_element_type=F32)
-
-    gc_acc[...] = context_part(0)
 
     @pl.loop(1, quarter)
     def _(u):
-        gc_acc[...] += context_part(u)
+        gc_acc[...] += context_part(u, half + 2 * u)
 
     def adam(total, cols):
         first = beta_one * m1[:, cols] + (1.0 - beta_one) * total
@@ -325,7 +352,7 @@
         def _():
             grad_peer_near(t - quarter).wait_recv()
             grad_mate(t).start()
-            gc_acc[...] += context_part(t)
+            gc_acc[...] += context_part(t, 2 * (t - quarter))
 
         @pl.when(t == half)
         def _():
@@ -368,8 +395,7 @@
 
         @pl.when(t < half)
         def _():
-            grad_mate(t).wait_recv()
-            grad_relay(t).wait_recv()
+            grad_chip(t).wait_recv()
             product = jnp.dot(ctxt[0], g4[t, 0:2 * tok], preferred_element_type=F32)
             product += jnp.dot(ctxt[1], g4[t, 2 * tok:4 * tok], preferred_element_type=F32)
             cut = product.shape[0] // 2
@@ -382,28 +408,21 @@
             grad_peer_far(t).wait_recv()
             grad_side(quarter + t).start()
 
+    def drain(block, sem):
+        remote(block, block, sem, st_r, peer_id()).wait_send()
+
     stat_send().wait_send()
-    ctx_mate().wait_send()
-    ctx_side().wait_send()
-    ctx_relay().wait_send()
-
-    @pl.loop(0, quarter)
-    def _(j):
-        grad_peer_near(j).wait_send()
-        grad_peer_far(j).wait_send()
-
-    for b in range(bits + 1):
-        gain_send(b).wait_send()
-
-    @pl.loop(0, half)
-    def _(i):
-        partial_send(i).wait_send()
-        grad_side(i).wait_send()
-        grad_mate(i).wait_send()
-        grad_relay(i).wait_send()
-        swap_send(i).wait_send()
-        for s in range(stages):
-            shard_send(s, i).wait_send()
+    drain(ctx.at[pl.ds(0, 3 * tok)], cx_s)
+    drain(psend, ps_s)
+    drain(gx.at[pl.ds(0, quarter)], gy_s.at[0])
+    drain(gx.at[pl.ds(0, quarter)], gy_s.at[1])
+    drain(gx, gx_s)
+    drain(gx, gm_s.at[0])
+    drain(gx, gm_s.at[1])
+    drain(gp, gg_s)
+    drain(fsend, fx_s)
+    for s in range(stages):
+        drain(sends[s], rs_s.at[s])
 
 
 def settle(nw, n1, n2, gg, gc, nw_out, n1_out, n2_out, gg_out, gc_out, flat, sem):
@@ -461,12 +480,11 @@
         vmem((tok, heads), F32),
         vmem((bits + 1, half, 1, cw), F32),
         vmem((bits + 1, half, 1, cw), F32),
-        dma((2,)), dma((chunks,)), dma((half,)), dma((3,)),
-        dma((half,)), dma((half,)), dma, dma, dma((3,)), dma((3,)),
-        dma((half,)), dma((half,)), dma((half,)), dma((half,)),
-        dma((half,)), dma((half,)), dma((half,)), dma((half,)),
-        dma((stages, half)), dma((stages, half)), dma((half,)), dma((half,)),
-        dma((bits + 1,)), dma((bits + 1,)),
+        dma((2,)), dma((3,)), dma, dma((3,)),
+        dma, dma((half,)), dma, dma, dma, dma((3,)),
+        dma((2,)), dma((half,)), dma, dma((half,)), dma((2,)), dma((half,)),
+        dma((stages,)), dma((stages, half)), dma, dma((half,)),
+        dma, dma((bits + 1,)),
     ]
     anywhere = pl.BlockSpec(memory_space=pltpu.HBM)
     pin = functools.partial(pltpu.with_memory_space_constraint, memory_space=pltpu.HBM)

time: 83.3 us -> 80.8 us (0.970)
  Pallas kernels: 82.5 us -> 80 us
    pallas_call x1, Pallas kernels: 80.8 us -> 78.4 us  [per_device(): pl.pallas_call(functools.partial(kernel, cfg), out_shape=(jax.ShapeDtypeS...]
where the time goes in v3:
time: 80.8 us; the launch traced here: 80.7 us
  Pallas kernels  80 us (99%)
    pallas_call x1, Pallas kernels, per_device(): pl.pallas_call(functools.partial(kernel, cfg), out_shape=(jax.ShapeDtypeS...  78.4 us
    pallas_call x1, Pallas kernels, per_device(): pl.pallas_call(settle, out_shape=(jax.ShapeDtypeStruct(first_moment.shape...  1.64 us

profile of v3, /device:TPU:0, one launch (start us, length us, event | category | flops | bytes accessed | tf_op | source)
XLA Modules:
  0.0 80.7 jit_solution(16457807603913896713)
XLA Ops:
  0.6 78.4 %shard_map.101 = (bf16[1,64,3584]{2,1,0:T(8,128)(2,1)S(1)}, f32[1,64,3584]{2,1,0:T(8,128)S(1)}, f32[1,64,3584]{2,1,0:T(8,128)S(1)}, f32[28,1,128]{2,1,0:T(1,128)S(1)}, bf16[320,1024]{1,0:T(8,128)(2,1)S(1)}) custom-call(bf16[320,1024]{1,0:T(8,128)(2,1)} %ctx_hbm.1, bf16[1024,3584]{1,0:T(8,128)(2,1)} %w_hbm.1, bf16[320,3584]{1,0:T(8,128)(2,1)} %cot_hbm.1, ...), custom_call_target="tpu_custom_call" | custom-call | tf_op jit(solution)/shard_map/pallas_call | solution.py:491
  79.0 1.6 %shard_map.102 = (bf16[1,64,3584]{2,1,0:T(8,128)(2,1)}, f32[1,64,3584]{2,1,0:T(8,128)}, f32[1,64,3584]{2,1,0:T(8,128)}, f32[3584]{0:T(1024)}, bf16[320,1024]{1,0:T(8,128)(2,1)}) custom-call(bf16[1,64,3584]{2,1,0:T(8,128)(2,1)S(1)} %get-tuple-element.10.nw, f32[1,64,3584]{2,1,0:T(8,128)S(1)} %get-tuple-element.11.n1, ...), custom_call_target="tpu_custom_call" | custom-call | tf_op jit(solution)/shard_map/pallas_call | solution.py:507

commit v4 on v3

--- a/solution.py
+++ b/solution.py
@@ -20,6 +20,7 @@
 LAG = 3
 SWAP = 6
 FIRST = 2
+WARM = 3
 
 
 def kernel(
@@ -27,10 +28,10 @@
     ctx_hbm, w_hbm, cot_hbm, gain_hbm, m1_hbm, m2_hbm,
     nw, n1, n2, gfin, gc_out,
     wv, ctx, ctxt_all, ctxt, cot, gain_flat, gain, psend, precv, own, stat_s, stat_r, inverse_v, shift_v, g4, gx,
-    sends, recvs, keeps, fsend, frecv, m1, m2, master, gc_acc,
+    sends, recvs, keeps, fsend, frecv, fkeep, m1, m2, master, gc_acc,
     gp, gpr,
     in_sem, w_sem, cot_sem, m_sem,
-    ps_s, ps_r, st_s, st_r, cx_s, cx_r, gy_s, gy_r, gx_s, gx_r, gm_s, gm_r,
+    ps_s, ps_r, st_s, st_r, cx_s, cx_r, gy_s, gx_s, gx_r, gm_s, gm_r,
     rs_s, rs_r, fx_s, fx_r, gg_s, gg_r,
 ):
     n, bits, quarter, cw, rows, tok, heads, width = cfg
@@ -122,12 +123,12 @@
     def grad_peer_near(j):
         return remote(
             g4.at[j, pl.ds(0, tok)], g4.at[quarter + j, pl.ds(0, tok)],
-            gy_s.at[0], gy_r.at[j], peer_id(),
+            gy_s.at[0], ps_r.at[j], peer_id(),
         )
 
     def grad_peer_far(j):
         return remote(
-            gx.at[j], gx.at[quarter + j], gy_s.at[1], gy_r.at[quarter + j], peer_id()
+            gx.at[j], gx.at[quarter + j], gy_s.at[1], ps_r.at[quarter + j], peer_id()
         )
 
     def grad_side(i):
@@ -154,7 +155,11 @@
         )
 
     def swap_send(i):
-        return remote(fsend.at[i], frecv.at[i], fx_s, fx_r.at[i], bit_id(1))
+        other = jnp.where(i < 2, 1 - i, i)
+        return remote(fsend.at[i], frecv.at[other], fx_s, fx_r.at[other], bit_id(1))
+
+    def swap_wait(i):
+        remote(fsend.at[i], frecv.at[i], fx_s, fx_r.at[i], bit_id(1)).wait_recv()
 
     steps = [0, *order]
 
@@ -292,16 +297,23 @@
         gp[0, spot - half * mp] = jnp.sum(upstream * normed, axis=0, keepdims=True)
         return (inverse * (upstream * gain[spot] - normed * shift_v[...])).astype(BF16)
 
+    gx[0] = gradient(1, 0)
+    g4[0, 2 * tok:3 * tok] = gx[0]
+    grad_relay(0).start()
+    grad_peer_far(0).start()
+    g4[0, 0:tok] = gradient(0, 0)
+    grad_mate(0).start()
+
     def far_part(j):
         gx[j] = gradient(1, j)
         grad_side(j).start()
         grad_peer_far(j).start()
 
-    @pl.loop(0, FIRST)
+    @pl.loop(1, FIRST)
     def _(j):
         far_part(j)
 
-    @pl.loop(0, quarter)
+    @pl.loop(1, quarter)
     def _(j):
         g4[j, 0:tok] = gradient(0, j)
         grad_mate(j).start()
@@ -323,9 +335,28 @@
     def _(j):
         grad_peer_near(j).start()
 
-    @pl.loop(1, quarter)
+    def context_add(u):
+        gc_acc[...] += context_part(u, half + 2 * u)
+
+    @pl.loop(1, WARM)
     def _(u):
-        gc_acc[...] += context_part(u, half + 2 * u)
+        context_add(u)
+
+    def split(slot, product):
+        cut = product.shape[0] // 2
+        sends[0][slot] = product[:cut].astype(BF16)
+        shard_send(0, slot).start()
+        keeps[0][slot] = product[cut:]
+
+    grad_chip(0).wait_recv()
+    for slot in range(2):
+        split(slot, jnp.dot(
+            ctxt[0], g4[0, 2 * slot * tok:2 * (slot + 1) * tok], preferred_element_type=F32
+        ))
+
+    @pl.loop(WARM, quarter)
+    def _(u):
+        context_add(u)
 
     def adam(total, cols):
         first = beta_one * m1[:, cols] + (1.0 - beta_one) * total
@@ -341,7 +372,7 @@
 
     swap_lag = LAG * stages + SWAP
 
-    @pl.loop(0, max(half + swap_lag, 3 * bits + 3))
+    @pl.loop(1, max(half + swap_lag, 3 * bits + 6))
     def _(t):
         @pl.when(t < half)
         def _():
@@ -359,7 +390,7 @@
             gc_out[...] = gc_acc[...].astype(BF16)
 
         for b in range(bits + 1):
-            @pl.when(t == 3 * b + 1)
+            @pl.when(t == 3 * b + 1 + 3 * (b >= bits - 1) + (b == bits))
             def _():
                 gain_send(b).wait_recv()
                 if b < bits:
@@ -369,17 +400,26 @@
                     gfin[pl.ds(mp * half, half)] = gp[bits]
                     gfin[pl.ds(peer * half, half)] = gpr[bits]
 
-        late_swap = t - swap_lag
-
-        @pl.when((late_swap >= 0) & (late_swap < half))
+        late_swap = t + 1 - swap_lag
+
+        @pl.when((late_swap >= 0) & (late_swap <= half))
         def _():
-            swap_send(late_swap).wait_recv()
-            adam(frecv[late_swap].astype(F32), cols_of(1, late_swap))
+            swap_wait(late_swap)
+            total = frecv[late_swap].astype(F32)
+
+            @pl.when(late_swap < 2)
+            def _():
+                first = jnp.where(late_swap == 0, starts[0], starts[2])
+                adam(total + fkeep[late_swap], pl.ds(pl.multiple_of(first * cw, cw), cw))
+
+            @pl.when(late_swap >= 2)
+            def _():
+                adam(total, cols_of(1, late_swap - 1))
 
         for s in range(stages - 1, -1, -1):
-            i = t - LAG * (s + 1)
-
-            @pl.when((i >= 0) & (i < half))
+            i = t + 1 - LAG * (s + 1)
+
+            @pl.when((i >= 0) & (i <= half))
             def _():
                 shard_send(s, i).wait_recv()
                 total = keeps[s][i] + recvs[s][i].astype(F32)
@@ -391,22 +431,26 @@
                 else:
                     fsend[i] = total[:cut].astype(BF16)
                     swap_send(i).start()
-                    adam(total[cut:], cols_of(0, i))
+
+                    @pl.when(i < 2)
+                    def _():
+                        fkeep[i] = total[cut:]
+
+                    @pl.when(i >= 2)
+                    def _():
+                        adam(total[cut:], cols_of(0, i - 1))
 
         @pl.when(t < half)
         def _():
             grad_chip(t).wait_recv()
             product = jnp.dot(ctxt[0], g4[t, 0:2 * tok], preferred_element_type=F32)
             product += jnp.dot(ctxt[1], g4[t, 2 * tok:4 * tok], preferred_element_type=F32)
-            cut = product.shape[0] // 2
-            sends[0][t] = product[:cut].astype(BF16)
-            shard_send(0, t).start()
-            keeps[0][t] = product[cut:]
-
-        @pl.when(t < quarter)
+            split(t + 1, product)
+
+        @pl.when(t <= quarter)
         def _():
-            grad_peer_far(t).wait_recv()
-            grad_side(quarter + t).start()
+            grad_peer_far(t - 1).wait_recv()
+            grad_side(quarter + t - 1).start()
 
     def drain(block, sem):
         remote(block, block, sem, st_r, peer_id()).wait_send()
@@ -416,7 +460,7 @@
     drain(psend, ps_s)
     drain(gx.at[pl.ds(0, quarter)], gy_s.at[0])
     drain(gx.at[pl.ds(0, quarter)], gy_s.at[1])
-    drain(gx, gx_s)
+    drain(gx.at[pl.ds(0, half - 1)], gx_s)
     drain(gx, gm_s.at[0])
     drain(gx, gm_s.at[1])
     drain(gp, gg_s)
@@ -469,11 +513,12 @@
         vmem((tok, cw), F32),
         vmem((half, 4 * tok, cw), BF16),
         vmem((half, tok, cw), BF16),
-        tuple(vmem((half, size, cw), BF16) for size in sizes),
-        tuple(vmem((half, size, cw), BF16) for size in sizes),
-        tuple(vmem((half, size, cw), F32) for size in sizes),
-        vmem((half, rows, cw), BF16),
-        vmem((half, rows, cw), BF16),
+        tuple(vmem((half + 1, size, cw), BF16) for size in sizes),
+        tuple(vmem((half + 1, size, cw), BF16) for size in sizes),
+        tuple(vmem((half + 1, size, cw), F32) for size in sizes),
+        vmem((half + 1, rows, cw), BF16),
+        vmem((half + 1, rows, cw), BF16),
+        vmem((2, rows, cw), F32),
         vmem((rows, width), F32),
         vmem((rows, width), F32),
         vmem((rows, width), BF16),
@@ -482,8 +527,8 @@
         vmem((bits + 1, half, 1, cw), F32),
         dma((2,)), dma((3,)), dma, dma((3,)),
         dma, dma((half,)), dma, dma, dma, dma((3,)),
-        dma((2,)), dma((half,)), dma, dma((half,)), dma((2,)), dma((half,)),
-        dma((stages,)), dma((stages, half)), dma, dma((half,)),
+        dma((2,)), dma, dma((half,)), dma((2,)), dma((half,)),
+        dma((stages,)), dma((stages, half + 1)), dma, dma((half + 1,)),
         dma, dma((bits + 1,)),
     ]
     anywhere = pl.BlockSpec(memory_space=pltpu.HBM)

time: 80.8 us -> 79.2 us (0.980)
  Pallas kernels: 80 us -> 78.5 us
    pallas_call x1, Pallas kernels: 78.4 us -> 76.8 us  [per_device(): pl.pallas_call(functools.partial(kernel, cfg), out_shape=(jax.ShapeDtypeS...]
where the time goes in v4:
time: 79.2 us; the launch traced here: 79.1 us
  Pallas kernels  78.5 us (99%)
    pallas_call x1, Pallas kernels, per_device(): pl.pallas_call(functools.partial(kernel, cfg), out_shape=(jax.ShapeDtypeS...  76.8 us
    pallas_call x1, Pallas kernels, per_device(): pl.pallas_call(settle, out_shape=(jax.ShapeDtypeStruct(first_moment.shape...  1.64 us

profile of v4, /device:TPU:0, one launch (start us, length us, event | category | flops | bytes accessed | tf_op | source)
XLA Modules:
  0.0 79.1 jit_solution(1638059368330170209)
XLA Ops:
  0.6 76.8 %shard_map.101 = (bf16[1,64,3584]{2,1,0:T(8,128)(2,1)S(1)}, f32[1,64,3584]{2,1,0:T(8,128)S(1)}, f32[1,64,3584]{2,1,0:T(8,128)S(1)}, f32[28,1,128]{2,1,0:T(1,128)S(1)}, bf16[320,1024]{1,0:T(8,128)(2,1)S(1)}) custom-call(bf16[320,1024]{1,0:T(8,128)(2,1)} %ctx_hbm.1, bf16[1024,3584]{1,0:T(8,128)(2,1)} %w_hbm.1, bf16[320,3584]{1,0:T(8,128)(2,1)} %cot_hbm.1, ...), custom_call_target="tpu_custom_call" | custom-call | tf_op jit(solution)/shard_map/pallas_call | solution.py:536
  77.5 1.6 %shard_map.102 = (bf16[1,64,3584]{2,1,0:T(8,128)(2,1)}, f32[1,64,3584]{2,1,0:T(8,128)}, f32[1,64,3584]{2,1,0:T(8,128)}, f32[3584]{0:T(1024)}, bf16[320,1024]{1,0:T(8,128)(2,1)}) custom-call(bf16[1,64,3584]{2,1,0:T(8,128)(2,1)S(1)} %get-tuple-element.10.nw, f32[1,64,3584]{2,1,0:T(8,128)S(1)} %get-tuple-element.11.n1, ...), custom_call_target="tpu_custom_call" | custom-call | tf_op jit(solution)/shard_map/pallas_call | solution.py:552

commit v5 on v4

--- a/solution.py
+++ b/solution.py
@@ -21,6 +21,7 @@
 SWAP = 6
 FIRST = 2
 WARM = 3
+MERGE = 4
 
 
 def kernel(
@@ -38,6 +39,7 @@
     half = 2 * quarter
     chunks = 4 * quarter
     stages = bits - 2
+    merged = half + 1 - MERGE
     dp, mp = lax.axis_index("dp"), lax.axis_index("mp")
     peer = 1 - mp
     side = (dp // 2) % 2
@@ -154,6 +156,14 @@
             sends[s].at[i], recvs[s].at[i], rs_s.at[s], rs_r.at[s, i], bit_id(order[s])
         )
 
+    def last_send(i, across):
+        part = pl.ds(rows * (1 - across), rows)
+        device = flip(dp, order[stages - 1])
+        return remote(
+            sends[-1].at[i, part], recvs[-1].at[i, part], rs_s.at[stages - 1], rs_r.at[stages - 1, i],
+            (flip(device, 1) if across else device, mp),
+        )
+
     def swap_send(i):
         other = jnp.where(i < 2, 1 - i, i)
         return remote(fsend.at[i], frecv.at[other], fx_s, fx_r.at[other], bit_id(1))
@@ -172,6 +182,9 @@
     for bit in range(bits - 1, -1, -1):
         pl.semaphore_signal(barrier, inc=1, device_id=bit_id(bit), device_id_type=MESH)
 
+    diagonal = (flip(flip(dp, order[stages - 1]), 1), mp)
+    pl.semaphore_signal(barrier, inc=1, device_id=diagonal, device_id_type=MESH)
+
     ctx_copy().start()
     w_copy(1, 0, w_sem.at[0]).start()
     w_copy(3, 0, w_sem.at[0]).start()
@@ -203,7 +216,7 @@
         w_copy(2, j, w_sem.at[2]).start()
 
     partial(0)
-    pl.semaphore_wait(barrier, bits + 1)
+    pl.semaphore_wait(barrier, bits + 2)
 
     partial_start(0)
     w_wait(2, half, w_sem.at[1])
@@ -338,7 +351,9 @@
     def context_add(u):
         gc_acc[...] += context_part(u, half + 2 * u)
 
-    @pl.loop(1, WARM)
+    warm = 1 + (WARM - 1) * (dp % 2)
+
+    @pl.loop(1, warm)
     def _(u):
         context_add(u)
 
@@ -354,7 +369,7 @@
             ctxt[0], g4[0, 2 * slot * tok:2 * (slot + 1) * tok], preferred_element_type=F32
         ))
 
-    @pl.loop(WARM, quarter)
+    @pl.loop(warm, quarter)
     def _(u):
         context_add(u)
 
@@ -412,9 +427,13 @@
                 first = jnp.where(late_swap == 0, starts[0], starts[2])
                 adam(total + fkeep[late_swap], pl.ds(pl.multiple_of(first * cw, cw), cw))
 
-            @pl.when(late_swap >= 2)
+            @pl.when((late_swap >= 2) & (late_swap < merged))
             def _():
                 adam(total, cols_of(1, late_swap - 1))
+
+            @pl.when(late_swap >= merged)
+            def _():
+                adam(total + recvs[-1][late_swap, 0:rows].astype(F32), cols_of(1, late_swap - 1))
 
         for s in range(stages - 1, -1, -1):
             i = t + 1 - LAG * (s + 1)
@@ -426,11 +445,26 @@
                 cut = total.shape[0] // 2
                 if s < stages - 1:
                     sends[s + 1][i] = total[:cut].astype(BF16)
-                    shard_send(s + 1, i).start()
+                    if s < stages - 2:
+                        shard_send(s + 1, i).start()
+                    else:
+                        @pl.when(i < merged)
+                        def _():
+                            shard_send(s + 1, i).start()
+
+                        @pl.when(i >= merged)
+                        def _():
+                            last_send(i, 1).start()
+                            last_send(i, 0).start()
+                            fsend[i] = total[cut:cut + rows].astype(BF16)
+                            swap_send(i).start()
+
                     keeps[s + 1][i] = total[cut:]
                 else:
-                    fsend[i] = total[:cut].astype(BF16)
-                    swap_send(i).start()
+                    @pl.when(i < merged)
+                    def _():
+                        fsend[i] = total[:cut].astype(BF16)
+                        swap_send(i).start()
 
                     @pl.when(i < 2)
                     def _():

time: 79.2 us -> 77.7 us (0.981)
  Pallas kernels: 78.5 us -> 76.9 us
    pallas_call x1, Pallas kernels: 76.8 us -> 75.2 us  [per_device(): pl.pallas_call(functools.partial(kernel, cfg), out_shape=(jax.ShapeDtypeS...]
where the time goes in v5:
time: 77.7 us; the launch traced here: 77.5 us
  Pallas kernels  76.9 us (99%)
    pallas_call x1, Pallas kernels, per_device(): pl.pallas_call(functools.partial(kernel, cfg), out_shape=(jax.ShapeDtypeS...  75.2 us
    pallas_call x1, Pallas kernels, per_device(): pl.pallas_call(settle, out_shape=(jax.ShapeDtypeStruct(first_moment.shape...  1.64 us

profile of v5, /device:TPU:0, one launch (start us, length us, event | category | flops | bytes accessed | tf_op | source)
XLA Modules:
  0.0 77.5 jit_solution(14209485929366050380)
XLA Ops:
  0.6 75.2 %shard_map.101 = (bf16[1,64,3584]{2,1,0:T(8,128)(2,1)S(1)}, f32[1,64,3584]{2,1,0:T(8,128)S(1)}, f32[1,64,3584]{2,1,0:T(8,128)S(1)}, f32[28,1,128]{2,1,0:T(1,128)S(1)}, bf16[320,1024]{1,0:T(8,128)(2,1)S(1)}) custom-call(bf16[320,1024]{1,0:T(8,128)(2,1)} %ctx_hbm.1, bf16[1024,3584]{1,0:T(8,128)(2,1)} %w_hbm.1, bf16[320,3584]{1,0:T(8,128)(2,1)} %cot_hbm.1, ...), custom_call_target="tpu_custom_call" | custom-call | tf_op jit(solution)/shard_map/pallas_call | solution.py:570
  75.9 1.6 %shard_map.102 = (bf16[1,64,3584]{2,1,0:T(8,128)(2,1)}, f32[1,64,3584]{2,1,0:T(8,128)}, f32[1,64,3584]{2,1,0:T(8,128)}, f32[3584]{0:T(1024)}, bf16[320,1024]{1,0:T(8,128)(2,1)}) custom-call(bf16[1,64,3584]{2,1,0:T(8,128)(2,1)S(1)} %get-tuple-element.10.nw, f32[1,64,3584]{2,1,0:T(8,128)S(1)} %get-tuple-element.11.n1, ...), custom_call_target="tpu_custom_call" | custom-call | tf_op jit(solution)/shard_map/pallas_call | solution.py:586

commit v6 on v5

--- a/solution.py
+++ b/solution.py
@@ -22,6 +22,7 @@
 FIRST = 2
 WARM = 3
 MERGE = 4
+MIX = 3
 
 
 def kernel(
@@ -187,7 +188,7 @@
 
     ctx_copy().start()
     w_copy(1, 0, w_sem.at[0]).start()
-    w_copy(3, 0, w_sem.at[0]).start()
+    w_copy(3, 0, w_sem.at[3]).start()
 
     def pair(base, j):
         right = jnp.concatenate([wv[base + 2 * j], wv[base + 2 * j + 1]], axis=1)
@@ -203,22 +204,31 @@
         partial_send(quarter + j).start()
 
     ctx_copy().wait()
-    w_wait(0, 2, w_sem.at[0])
+    w_wait(0, 1, w_sem.at[0])
+
+    def partial_first(far):
+        value = jnp.dot(ctx[0:tok], wv[far], preferred_element_type=F32)
+        psend[far * quarter] = value.astype(BF16)
+
+    partial_first(0)
+    pl.semaphore_wait(barrier, bits + 2)
+
+    partial_send(0).start()
 
     @pl.loop(1, quarter)
     def _(j):
         w_copy(1, j, w_sem.at[1]).start()
         w_copy(3, j, w_sem.at[1]).start()
 
+    w_wait(1, 2, w_sem.at[3])
+    partial_first(1)
+    partial_send(quarter).start()
+
     @pl.loop(0, quarter)
     def _(j):
         w_copy(0, j, w_sem.at[2]).start()
         w_copy(2, j, w_sem.at[2]).start()
 
-    partial(0)
-    pl.semaphore_wait(barrier, bits + 2)
-
-    partial_start(0)
     w_wait(2, half, w_sem.at[1])
 
     @pl.loop(1, quarter)
@@ -326,48 +336,61 @@
     def _(j):
         far_part(j)
 
-    @pl.loop(1, quarter)
-    def _(j):
-        g4[j, 0:tok] = gradient(0, j)
-        grad_mate(j).start()
-
-    def context_part(u, base):
-        left = jnp.concatenate([g4[u, 0:tok], gx[u]], axis=1)
-        right = jnp.concatenate([wv[base], wv[base + 1]], axis=1)
-        return lax.dot_general(left, right, (((1,), (1,)), ((), ())), preferred_element_type=F32)
-
-    gc_acc[...] = context_part(0, half)
-
-    @pl.loop(FIRST, quarter)
-    def _(j):
-        far_part(j)
-
-    gain_send(0).start()
-
-    @pl.loop(0, quarter)
-    def _(j):
-        grad_peer_near(j).start()
-
-    def context_add(u):
-        gc_acc[...] += context_part(u, half + 2 * u)
-
-    warm = 1 + (WARM - 1) * (dp % 2)
-
-    @pl.loop(1, warm)
-    def _(u):
-        context_add(u)
-
     def split(slot, product):
         cut = product.shape[0] // 2
         sends[0][slot] = product[:cut].astype(BF16)
         shard_send(0, slot).start()
         keeps[0][slot] = product[cut:]
 
-    grad_chip(0).wait_recv()
-    for slot in range(2):
-        split(slot, jnp.dot(
-            ctxt[0], g4[0, 2 * slot * tok:2 * (slot + 1) * tok], preferred_element_type=F32
-        ))
+    def first_products():
+        grad_chip(0).wait_recv()
+        for slot in range(2):
+            split(slot, jnp.dot(
+                ctxt[0], g4[0, 2 * slot * tok:2 * (slot + 1) * tok], preferred_element_type=F32
+            ))
+
+    @pl.when(dp % 2 == 0)
+    def _():
+        first_products()
+
+    @pl.loop(1, quarter)
+    def _(j):
+        g4[j, 0:tok] = gradient(0, j)
+        grad_mate(j).start()
+
+    def context_part(u, base):
+        left = jnp.concatenate([g4[u, 0:tok], gx[u]], axis=1)
+        right = jnp.concatenate([wv[base], wv[base + 1]], axis=1)
+        return lax.dot_general(left, right, (((1,), (1,)), ((), ())), preferred_element_type=F32)
+
+    gc_acc[...] = context_part(0, half)
+
+    @pl.loop(FIRST, quarter)
+    def _(j):
+        far_part(j)
+
+        @pl.when(j >= quarter - MIX)
+        def _():
+            grad_peer_near(j - (quarter - MIX)).start()
+
+    gain_send(0).start()
+
+    @pl.loop(MIX, quarter)
+    def _(j):
+        grad_peer_near(j).start()
+
+    def context_add(u):
+        gc_acc[...] += context_part(u, half + 2 * u)
+
+    warm = 1 + (WARM - 1) * (dp % 2)
+
+    @pl.loop(1, warm)
+    def _(u):
+        context_add(u)
+
+    @pl.when(dp % 2 == 1)
+    def _():
+        first_products()
 
     @pl.loop(warm, quarter)
     def _(u):
@@ -559,7 +582,7 @@
         vmem((tok, heads), F32),
         vmem((bits + 1, half, 1, cw), F32),
         vmem((bits + 1, half, 1, cw), F32),
-        dma((2,)), dma((3,)), dma, dma((3,)),
+        dma((2,)), dma((4,)), dma, dma((3,)),
         dma, dma((half,)), dma, dma, dma, dma((3,)),
         dma((2,)), dma, dma((half,)), dma((2,)), dma((half,)),
         dma((stages,)), dma((stages, half + 1)), dma, dma((half + 1,)),

time: 77.7 us -> 77.4 us (level)
  no operation moved by 1% of the time
where the time goes in v6:
time: 77.4 us; the launch traced here: 77.3 us
  Pallas kernels  76.6 us (99%)
    pallas_call x1, Pallas kernels, per_device(): pl.pallas_call(functools.partial(kernel, cfg), out_shape=(jax.ShapeDtypeS...  75 us
    pallas_call x1, Pallas kernels, per_device(): pl.pallas_call(settle, out_shape=(jax.ShapeDtypeStruct(first_moment.shape...  1.64 us

profile of v6, /device:TPU:0, one launch (start us, length us, event | category | flops | bytes accessed | tf_op | source)
XLA Modules:
  0.0 77.3 jit_solution(7857396148837565)
XLA Ops:
  0.6 75.0 %shard_map.101 = (bf16[1,64,3584]{2,1,0:T(8,128)(2,1)S(1)}, f32[1,64,3584]{2,1,0:T(8,128)S(1)}, f32[1,64,3584]{2,1,0:T(8,128)S(1)}, f32[28,1,128]{2,1,0:T(1,128)S(1)}, bf16[320,1024]{1,0:T(8,128)(2,1)S(1)}) custom-call(bf16[320,1024]{1,0:T(8,128)(2,1)} %ctx_hbm.1, bf16[1024,3584]{1,0:T(8,128)(2,1)} %w_hbm.1, bf16[320,3584]{1,0:T(8,128)(2,1)} %cot_hbm.1, ...), custom_call_target="tpu_custom_call" | custom-call | tf_op jit(solution)/shard_map/pallas_call | solution.py:593
  75.6 1.6 %shard_map.102 = (bf16[1,64,3584]{2,1,0:T(8,128)(2,1)}, f32[1,64,3584]{2,1,0:T(8,128)}, f32[1,64,3584]{2,1,0:T(8,128)}, f32[3584]{0:T(1024)}, bf16[320,1024]{1,0:T(8,128)(2,1)}) custom-call(bf16[1,64,3584]{2,1,0:T(8,128)(2,1)S(1)} %get-tuple-element.10.nw, f32[1,64,3584]{2,1,0:T(8,128)S(1)} %get-tuple-element.11.n1, ...), custom_call_target="tpu_custom_call" | custom-call | tf_op jit(solution)/shard_map/pallas_call | solution.py:609

commit v7 on v6

--- a/solution.py
+++ b/solution.py
@@ -299,7 +299,7 @@
     square = jnp.sum(square, axis=1, keepdims=True)
     cross = jnp.sum(cross, axis=1, keepdims=True)
     even = lax.broadcasted_iota(jnp.int32, (tok, 128), 1) % 2 == 0
-    stat_s[...] = jnp.transpose(jnp.where(even, square, cross))[0:8]
+    stat_s[...] = jnp.transpose(jnp.where(even, square, cross))[0:2]
     stat_send().start()
     stat_send().wait_recv()
     totals = stat_s[...] + stat_r[...]
@@ -564,8 +564,8 @@
         vmem((half, tok, cw), BF16),
         vmem((half, tok, cw), BF16),
         vmem((half, tok, cw), F32),
-        vmem((8, tok), F32),
-        vmem((8, tok), F32),
+        vmem((2, tok), F32),
+        vmem((2, tok), F32),
         vmem((tok, cw), F32),
         vmem((tok, cw), F32),
         vmem((half, 4 * tok, cw), BF16),

time: 77.4 us -> 77.3 us (level)
  no operation moved by 1% of the time
where the time goes in v7:
time: 77.3 us; the launch traced here: 77.1 us
  Pallas kernels  76.5 us (99%)
    pallas_call x1, Pallas kernels, per_device(): pl.pallas_call(functools.partial(kernel, cfg), out_shape=(jax.ShapeDtypeS...  74.9 us
    pallas_call x1, Pallas kernels, per_device(): pl.pallas_call(settle, out_shape=(jax.ShapeDtypeStruct(first_moment.shape...  1.64 us

profile of v7, /device:TPU:0, one launch (start us, length us, event | category | flops | bytes accessed | tf_op | source)
XLA Modules:
  0.0 77.1 jit_solution(16042307331312354194)
XLA Ops:
  0.6 74.9 %shard_map.101 = (bf16[1,64,3584]{2,1,0:T(8,128)(2,1)S(1)}, f32[1,64,3584]{2,1,0:T(8,128)S(1)}, f32[1,64,3584]{2,1,0:T(8,128)S(1)}, f32[28,1,128]{2,1,0:T(1,128)S(1)}, bf16[320,1024]{1,0:T(8,128)(2,1)S(1)}) custom-call(bf16[320,1024]{1,0:T(8,128)(2,1)} %ctx_hbm.1, bf16[1024,3584]{1,0:T(8,128)(2,1)} %w_hbm.1, bf16[320,3584]{1,0:T(8,128)(2,1)} %cot_hbm.1, ...), custom_call_target="tpu_custom_call" | custom-call | tf_op jit(solution)/shard_map/pallas_call | solution.py:593
  75.5 1.6 %shard_map.102 = (bf16[1,64,3584]{2,1,0:T(8,128)(2,1)}, f32[1,64,3584]{2,1,0:T(8,128)}, f32[1,64,3584]{2,1,0:T(8,128)}, f32[3584]{0:T(1024)}, bf16[320,1024]{1,0:T(8,128)(2,1)}) custom-call(bf16[1,64,3584]{2,1,0:T(8,128)(2,1)S(1)} %get-tuple-element.10.nw, f32[1,64,3584]{2,1,0:T(8,128)S(1)} %get-tuple-element.11.n1, ...), custom_call_target="tpu_custom_call" | custom-call | tf_op jit(solution)/shard_map/pallas_call | solution.py:609
